TPU v7x, 32 devices: a whole 2x2x4 slice. The times are simulated.
32 devices in a mesh: row: 8 (over y, x, core), col: 4 (over z).
Axes of the slice: x: 2, y: 2, z: 4, core: 2. Of those that a mesh axis runs over, the one named last changes fastest.
Arguments:
- front_tiles: float32 [2, 2048, 2, 1024], P(None, 'row', None, 'col'), may hold values from -6 to 6, as said below
- lead_tiles: int32 [2, 8], P(None, 'row'), may hold values from 0 to 7
- damping: float32 [2, 1024], P(None, 'col'), may hold values from 1.5 to 6
Outputs:
- factor: float32 [2, 2048, 2, 1024], P(None, 'row', None, 'col')
Inputs may be any that keep to these rules, and one draw needn't show every extreme that they name: `front_tiles`: the front's entries. `lead_tiles`: entries of the first 8 tile rows are not read.
All inputs are finite; a program needn't handle non-finite values.
Results may differ from a plain program's by a relative error of at most 0.00005.
Values sent between devices are 32-bit elements; how exact they have to be, the bound alone decides.
No kernel may reach another device: no remote copies, remote signals or barrier semaphores. Data moves between devices by JAX's collectives and lax.ppermute only.
A program may use at most 64 MiB of HBM per device.

v0:
```python
import jax
import jax.numpy as jnp
from jax import lax
from jax.sharding import PartitionSpec as P

HIGHEST = lax.Precision.HIGHEST


def mm(a, b):
    return jnp.dot(a, b, precision=HIGHEST, preferred_element_type=jnp.float32)


def separator_tiles(sep_local, n_row, n_col, n_columns, after_first):
    sep_slots, tile, cslots, _ = sep_local.shape
    if sep_slots * n_row == n_columns:
        pieces = []
        for t in range(cslots):
            piece = sep_local[:, :, t, :].reshape(sep_slots * tile, tile)
            if t == 1:
                piece = piece + after_first(pieces[0])
            pieces.append(lax.all_gather(piece, ("row", "col"), axis=0))
        if cslots == 1:
            after_first(pieces[0])

        def get(i, j):
            g = pieces[j // n_col]
            row = (i // n_row) * tile
            return g[(i % n_row) * n_col + j % n_col, row:row + tile]

        return get
    after_first(None)
    g = lax.all_gather(sep_local, "row", axis=1, tiled=True)
    g = g.reshape(sep_slots * n_row * tile, cslots, tile)[: n_columns * tile]
    g = lax.all_gather(g, "col", axis=2)

    def get(i, j):
        return g[i * tile:(i + 1) * tile, j // n_col, j % n_col, :]

    return get


def after(value):
    return value.reshape(-1)[0] * 0.0


def lower_inverse(lower):
    size = lower.shape[0]
    eye = jnp.eye(size, dtype=lower.dtype)
    diag = jnp.sum(lower * eye, axis=1)
    strict = jnp.tril(jnp.ones((size, size), jnp.bool_), -1)
    power = jnp.where(strict, -lower / diag[:, None], 0.0)
    product = eye + power
    span = 2
    while span < size:
        power = mm(power, power)
        product = mm(product, eye + power)
        span *= 2
    return product / diag[None, :]


def factor_diag(diag):
    half = diag.shape[0] // 2
    l00 = jnp.tril(lax.linalg.cholesky(diag[:half, :half], symmetrize_input=False))
    i00 = lower_inverse(l00)
    l10 = mm(diag[half:, :half], i00.T)
    s11 = diag[half:, half:] - mm(l10, l10.T)
    l11 = jnp.tril(lax.linalg.cholesky(s11, symmetrize_input=True))
    i11 = lower_inverse(l11)
    i10 = -mm(i11, mm(l10, i00))
    zero = jnp.zeros((half, half), diag.dtype)
    lkk = jnp.block([[l00, zero], [l10, l11]])
    linv = jnp.block([[i00, zero], [i10, i11]])
    return lkk, linv


def shards(front_tiles, lead_tiles, damping):
    slot_count, tile, col_slot_count, _ = front_tiles.shape
    n_row = lax.axis_size("row")
    n_col = lax.axis_size("col")
    row_at = lax.axis_index("row")
    col_at = lax.axis_index("col")
    n_columns = col_slot_count * n_col
    row_tiles = jnp.arange(slot_count, dtype=jnp.int32) * n_row + row_at
    col_tiles = jnp.arange(col_slot_count, dtype=jnp.int32) * n_col + col_at
    leads = jnp.where(row_tiles < n_columns, 0, lead_tiles[:, 0])
    kept_mask = col_tiles[None, :] >= leads[:, None]
    working = jnp.where(kept_mask[:, None, :, None], front_tiles, 0.0)
    identity = jnp.eye(tile, dtype=jnp.float32)
    on_diagonal = (row_tiles[:, None] == col_tiles[None, :])[:, None, :, None]
    damp_term = identity[None, :, None, :] * damping[None, None, :, :]
    working = working + jnp.where(on_diagonal, damp_term, 0.0)

    tail_first = n_columns // n_row
    n_tail = (slot_count - tail_first) * tile
    tail_pieces = []

    def gather_tail(first_piece):
        tail_local = working[tail_first:]
        if first_piece is not None:
            tail_local = tail_local + after(first_piece)
        for t in range(col_slot_count):
            piece = tail_local[:, :, t, :].reshape(n_tail, tile)
            tail_pieces.append(lax.all_gather(piece, "col", axis=0))
        return after(tail_pieces[-1])

    sep_slots = -(-n_columns // n_row)
    get_tile = separator_tiles(working[:sep_slots], n_row, n_col, n_columns, gather_tail)

    total_rows = n_columns * tile + n_tail
    factor = jnp.zeros((total_rows, n_columns * tile), jnp.float32)
    for k in range(n_columns):
        cols = slice(k * tile, (k + 1) * tile)
        parts = [get_tile(i, k) for i in range(k, n_columns)] + [tail_pieces[k // n_col][k % n_col]]
        panel = jnp.concatenate(parts, axis=0)
        if k > 0:
            left = factor[k * tile:, : k * tile]
            top = factor[k * tile:(k + 1) * tile, : k * tile]
            panel = panel - mm(left, top.T)
        diag = panel[:tile]
        diag = jnp.tril(diag) + jnp.tril(diag, -1).T
        lkk, linv = factor_diag(diag)
        below = mm(panel[tile:], linv.T)
        factor = factor.at[k * tile:, cols].set(jnp.concatenate([lkk, below], axis=0))

    outs = []
    for slot in range(slot_count):
        tile_row = slot * n_row + row_at
        if slot < tail_first:
            start = tile_row * tile
        else:
            tail_start = n_columns * tile + (slot - tail_first) * tile
            start = jnp.where(tile_row < n_columns, tile_row * tile, tail_start)
        picked = lax.dynamic_slice_in_dim(factor, start, tile, axis=0)
        picked = picked.reshape(tile, col_slot_count, n_col, tile)
        picked = lax.dynamic_index_in_dim(picked, col_at, axis=2, keepdims=False)
        outs.append(picked)
    return jnp.stack(outs, axis=0)


def solution(mesh):
    in_specs = (P(None, "row", None, "col"), P(None, "row"), P(None, "col"))
    out_specs = P(None, "row", None, "col")
    return jax.shard_map(shards, mesh=mesh, in_specs=in_specs, out_specs=out_specs, check_vma=False)
```

profile of v0, /device:TPU:0, one launch (start us, length us, event | category | flops | bytes accessed | tf_op | source)
XLA Modules:
  0.0 584.0 jit_solution(6537366342205130301)
XLA Ops:
  11.0 79.5 %all-gather.9.cloned.1.call-done = f32[32,256,1,256]{3,1,2,0:T(8,128)} async-done(((f32[1,256,1,256]{3,1,2,0:T(8,128)}), f32[32,256,1,256]{3,1,2,0:T(8,128)}) %all-gather.9.cloned.1.call-update) | async-done | bytes 8388624 | tf_op jit(solution)/shard_map/all_gather | solution.py:21
  90.5 4.4 fusion.310
  96.2 11.7 %custom-call.18 = f32[128,128]{1,0:T(8,128)S(1)} custom-call(f32[128,128]{1,0:T(8,128)S(1)} %copy.252), custom_call_target="Cholesky" | custom-call | tf_op jit(solution)/shard_map/cholesky/custom-call.1 | solution.py:63
  113.7 11.7 %custom-call.19 = f32[128,128]{1,0:T(8,128)S(1)} custom-call(f32[128,128]{1,0:T(8,128)S(1)} %copy.256), custom_call_target="Cholesky" | custom-call | tf_op jit(solution)/shard_map/cholesky/custom-call.1 | solution.py:67
  131.1 1.8 copy.401
  136.4 1.8 copy.404
  138.2 1.8 copy.405
  141.8 12.5 %copy.481 = f32[1024,2,8,128]{3,1,2,0:T(2,128)S(1)} copy(f32[1024,2,8,128]{3,2,1,0:T(8,128)} %bitcast.482) | data formatting | bytes 16777216
  160.3 1.8 copy.408
  163.9 1.8 copy.409
  172.8 1.8 copy.415
  176.3 1.8 copy.416
  178.1 1.8 copy.417
  179.9 1.8 copy.418
  207.6 2.0 fusion.312
  210.7 1.9 fusion.82
  212.6 3.5 fusion.80
  217.8 2.1 convolution_subtract_fusion
  225.7 11.7 %custom-call.20 = f32[128,128]{1,0:T(8,128)S(1)} custom-call(f32[128,128]{1,0:T(8,128)S(1)} %copy.271), custom_call_target="Cholesky" | custom-call | tf_op jit(solution)/shard_map/cholesky/custom-call.1 | solution.py:63
  247.1 12.7 %custom-call.21 = f32[128,128]{1,0:T(8,128)S(1)} custom-call(f32[128,128]{1,0:T(8,128)} %copy.275), custom_call_target="Cholesky" | custom-call | tf_op jit(solution)/shard_map/cholesky/custom-call.1 | solution.py:67
  267.5 5.8 fusion.29
  273.3 8.9 %scatter.26 = f32[2304,2048]{1,0:T(8,128)} pad(f32[2304,256]{1,0:T(8,128)S(1)} %fusion.22, f32[]{:T(128)} %constant.351.clone.1), padding=0_0x0_1792 | pad | bytes 21233668 | tf_op jit(solution)/shard_map/scatter | solution.py:123
  284.1 3.1 fusion.24
  287.1 6.3 %fusion.18 = f32[1792,256]{0,1:T(8,128)S(1)} fusion(f32[1792,256]{0,1:T(8,128)} %bitcast_dynamic-update-slice_fusion.11, f32[2304,2048]{1,0:T(8,128)} %fusion.24), kind=kOutput, calls=%fused_computation.126 | convolution fusion | flops 2819031040 | bytes 7864320 | tf_op jit(solution)/shard_map/dot_general | solution.py:10
  293.9 11.7 %custom-call.22 = f32[128,128]{1,0:T(8,128)S(1)} custom-call(f32[128,128]{1,0:T(8,128)S(1)} %copy.289), custom_call_target="Cholesky" | custom-call | tf_op jit(solution)/shard_map/cholesky/custom-call.1 | solution.py:63
  314.3 11.7 %custom-call.23 = f32[128,128]{1,0:T(8,128)S(1)} custom-call(f32[128,128]{1,0:T(8,128)S(1)} %copy.293), custom_call_target="Cholesky" | custom-call | tf_op jit(solution)/shard_map/cholesky/custom-call.1 | solution.py:67
  332.9 2.7 fusion.34
  337.0 7.3 %fusion.15 = f32[1536,256]{0,1:T(8,128)S(1)} fusion(f32[1536,256]{0,1:T(8,128)} %bitcast_dynamic-update-slice_fusion.5, f32[2304,2048]{1,0:T(8,128)} %fusion.28), kind=kOutput, calls=%fused_computation.13 | convolution fusion | flops 3624271872 | bytes 8650752 | tf_op jit(solution)/shard_map/dot_general | solution.py:10
  344.7 11.7 %custom-call.24 = f32[128,128]{1,0:T(8,128)S(1)} custom-call(f32[128,128]{1,0:T(8,128)S(1)} %copy.306), custom_call_target="Cholesky" | custom-call | tf_op jit(solution)/shard_map/cholesky/custom-call.1 | solution.py:63
  362.2 12.3 %custom-call.25 = f32[128,128]{1,0:T(8,128)} custom-call(f32[128,128]{1,0:T(8,128)S(1)} %copy.310), custom_call_target="Cholesky" | custom-call | tf_op jit(solution)/shard_map/cholesky/custom-call.1 | solution.py:67
  384.2 2.3 fusion.42
  387.9 2.7 fusion.309
  392.9 7.9 %fusion.12 = f32[1280,256]{0,1:T(8,128)S(1)} fusion(f32[1280,256]{0,1:T(8,128)S(1)} %bitcast_dynamic-update-slice_fusion, f32[2304,2048]{1,0:T(8,128)} %fusion.33), kind=kOutput, calls=%fused_computation.12 | convolution fusion | flops 4026859520 | bytes 8912896 | tf_op jit(solution)/shard_map/dot_general | solution.py:10
  401.2 11.7 %custom-call.26 = f32[128,128]{1,0:T(8,128)S(1)} custom-call(f32[128,128]{1,0:T(8,128)S(1)} %copy.322), custom_call_target="Cholesky" | custom-call | tf_op jit(solution)/shard_map/cholesky/custom-call.1 | solution.py:63
  418.1 11.9 %custom-call.27 = f32[128,128]{1,0:T(8,128)S(1)} custom-call(f32[128,128]{1,0:T(8,128)S(1)} %copy.326), custom_call_target="Cholesky" | custom-call | tf_op jit(solution)/shard_map/cholesky/custom-call.1 | solution.py:67
  434.4 1.8 fusion.56
  437.4 6.8 %fusion.36 = f32[1024,256]{1,0:T(8,128)S(1)} fusion(f32[2304,2048]{1,0:T(8,128)} %fusion.41, f32[256,256]{1,0:T(8,128)S(1)} %copy-done.21, f32[256,256]{1,0:T(8,128)S(1)} %get-tuple-element.145, f32[256,256]{1,0:T(8,128)S(1)} %get-tuple-element.143, f32[256,256]{1,0:T(8,128)S(1)} %get-tuple-element.144), kind=kOutput, calls=%fused_computation.151 | convolution fusion | flops 4027580416 | bytes 8650752 | tf_op jit(solution)/shard_map/dot_general | solution.py:10
  444.6 11.7 %custom-call.28 = f32[128,128]{1,0:T(8,128)S(1)} custom-call(f32[128,128]{1,0:T(8,128)S(1)} %copy.332), custom_call_target="Cholesky" | custom-call | tf_op jit(solution)/shard_map/cholesky/custom-call.1 | solution.py:63
  461.5 11.7 %custom-call.29 = f32[128,128]{1,0:T(8,128)S(1)} custom-call(f32[128,128]{1,0:T(8,128)S(1)} %copy.336), custom_call_target="Cholesky" | custom-call | tf_op jit(solution)/shard_map/cholesky/custom-call.1 | solution.py:67
  480.4 7.1 %fusion.44 = f32[768,256]{0,1:T(8,128)S(1)} fusion(f32[2304,2048]{1,0:T(8,128)} %fusion.55, f32[256,256]{0,1:T(8,128)S(1)} %bitcast.490, f32[256,256]{0,1:T(8,128)S(1)} %bitcast.492, f32[256,256]{0,1:T(8,128)S(1)} %bitcast.491), kind=kOutput, calls=%fused_computation.159 | convolution fusion | flops 3624468480 | bytes 7864320 | tf_op jit(solution)/shard_map/dot_general | solution.py:10
  487.9 11.7 %custom-call.30 = f32[128,128]{1,0:T(8,128)S(1)} custom-call(f32[128,128]{1,0:T(8,128)S(1)} %copy.346), custom_call_target="Cholesky" | custom-call | tf_op jit(solution)/shard_map/cholesky/custom-call.1 | solution.py:63
  504.6 11.9 %custom-call.31 = f32[128,128]{1,0:T(8,128)S(1)} custom-call(f32[128,128]{1,0:T(8,128)S(1)} %fusion.229), custom_call_target="Cholesky" | custom-call | tf_op jit(solution)/shard_map/cholesky/custom-call.1 | solution.py:67
  523.1 5.9 %fusion.49 = f32[512,256]{0,1:T(8,128)S(1)} fusion(f32[2304,2048]{1,0:T(8,128)} %fusion.61, f32[256,256]{0,1:T(8,128)S(1)} %bitcast.489, f32[256,256]{0,1:T(8,128)S(1)} %bitcast.493), kind=kOutput, calls=%fused_computation.160 | convolution fusion | flops 2818834432 | bytes 6553600 | tf_op jit(solution)/shard_map/dot_general | solution.py:10
  529.4 11.9 %custom-call.32 = f32[128,128]{1,0:T(8,128)S(1)} custom-call(f32[128,128]{1,0:T(8,128)S(1)} %copy.357), custom_call_target="Cholesky" | custom-call | tf_op jit(solution)/shard_map/cholesky/custom-call.1 | solution.py:63
  546.4 11.7 %custom-call.33 = f32[128,128]{1,0:T(8,128)S(1)} custom-call(f32[128,128]{1,0:T(8,128)S(1)} %broadcast_multiply_fusion.1), custom_call_target="Cholesky" | custom-call | tf_op jit(solution)/shard_map/cholesky/custom-call.1 | solution.py:67
  564.1 3.9 constant_dynamic-slice_fusion.3
  568.0 2.9 copy.364
  572.3 1.9 copy.366
  (518 shorter events, 177.3 us)
Async XLA Ops:
  6.5 83.9 %all-gather.9.cloned.1.call-start = ((), (), s32[]{:S(2)}) async-start(), calls=%async_computation | async-start | bytes 8650752 | tf_op jit(solution)/shard_map/all_gather | solution.py:21
  10.2 197.3 %all-gather.11.cloned.1.call-start = ((), (), s32[]{:S(2)}) async-start(), calls=%async_computation.1 | async-start | bytes 1310720 | tf_op jit(solution)/shard_map/all_gather | solution.py:103
  109.3 0.6 copy-start.25
  126.8 0.6 copy-start.27
  156.5 151.3 %all-gather.13.cloned.1.call-start = ((), (), s32[]{:S(2)}) async-start(), calls=%async_computation.2 | async-start | bytes 1310720 | tf_op jit(solution)/shard_map/all_gather | solution.py:103
  182.5 4.2 copy-start.11
  182.5 4.2 copy-start.10
  182.5 5.4 copy-start.19
  182.5 6.2 %copy-start.20 = (f32[1,256,1,256]{1,3,2,0:T(8,128)S(1)}, f32[1,256,1,256]{1,3,2,0:T(8,128)}, u32[]{:S(2)}) copy-start(f32[1,256,1,256]{1,3,2,0:T(8,128)} %copy.410) | copy-start | bytes 786436
  182.5 7.0 %copy-start.18 = (f32[1,256,1,256]{1,3,2,0:T(8,128)S(1)}, f32[1,256,1,256]{1,3,2,0:T(8,128)}, u32[]{:S(2)}) copy-start(f32[1,256,1,256]{1,3,2,0:T(8,128)} %copy.411) | copy-start | bytes 786436
  183.6 6.7 %copy-start.34 = (f32[128,128]{1,0:T(8,128)S(1)}, f32[128,128]{1,0:T(8,128)}, u32[]{:S(2)}) copy-start(f32[128,128]{1,0:T(8,128)} %fusion.322) | copy-start | bytes 196612
  184.6 6.5 %copy-start.13 = (f32[1,256,1,256]{1,3,2,0:T(8,128)S(1)}, f32[1,256,1,256]{1,3,2,0:T(8,128)}, u32[]{:S(2)}) copy-start(f32[1,256,1,256]{1,3,2,0:T(8,128)} %copy.412) | copy-start | bytes 786436
  185.7 6.2 %copy-start.12 = (f32[1,256,1,256]{1,3,2,0:T(8,128)S(1)}, f32[1,256,1,256]{1,3,2,0:T(8,128)}, u32[]{:S(2)}) copy-start(f32[1,256,1,256]{1,3,2,0:T(8,128)} %copy.413) | copy-start | bytes 786436
  186.7 6.0 %copy-start.16 = (f32[1,256,1,256]{1,3,2,0:T(8,128)S(1)}, f32[1,256,1,256]{1,3,2,0:T(8,128)}, u32[]{:S(2)}) copy-start(f32[1,256,1,256]{1,3,2,0:T(8,128)} %copy.416) | copy-start | bytes 786436
  186.8 6.6 %copy-start.17 = (f32[1,256,1,256]{1,3,2,0:T(8,128)S(1)}, f32[1,256,1,256]{1,3,2,0:T(8,128)}, u32[]{:S(2)}) copy-start(f32[1,256,1,256]{1,3,2,0:T(8,128)} %copy.417) | copy-start | bytes 786436
  186.8 7.3 %copy-start.14 = (f32[1,256,1,256]{1,3,2,0:T(8,128)S(1)}, f32[1,256,1,256]{1,3,2,0:T(8,128)}, u32[]{:S(2)}) copy-start(f32[1,256,1,256]{1,3,2,0:T(8,128)} %copy.418) | copy-start | bytes 786436
  188.0 7.0 %copy-start.15 = (f32[1,256,1,256]{1,3,2,0:T(8,128)S(1)}, f32[1,256,1,256]{1,3,2,0:T(8,128)}, u32[]{:S(2)}) copy-start(f32[1,256,1,256]{1,3,2,0:T(8,128)} %copy.419) | copy-start | bytes 786436
  195.7 192.1 %all-gather.15.cloned.1.call-start = ((), (), s32[]{:S(2)}) async-start(), calls=%async_computation.3 | async-start | bytes 8650752 | tf_op jit(solution)/shard_map/all_gather | solution.py:21
  210.7 1.9 copy-start.2
  212.6 3.6 copy-start.26
  212.6 3.6 copy-start.28
  212.6 3.6 copy-start.29
  216.1 1.6 copy-start.3
  219.9 1.4 copy-start
  224.9 0.7 copy-start.22
  237.4 4.2 copy-start.23
  238.8 0.6 copy-start.30
  241.6 0.6 copy-start.24
  261.3 0.6 copy-start.32
  273.3 10.8 %copy-start.31 = (f32[128,128]{1,0:T(8,128)S(1)}, f32[128,128]{1,0:T(8,128)}, u32[]{:S(2)}) copy-start(f32[128,128]{1,0:T(8,128)} %copy-done.30) | copy-start | bytes 196612
  273.3 10.8 %copy-start.33 = (f32[128,128]{1,0:T(8,128)S(1)}, f32[128,128]{1,0:T(8,128)}, u32[]{:S(2)}) copy-start(f32[128,128]{1,0:T(8,128)} %copy-done.32) | copy-start | bytes 196612
  344.6 29.9 %copy-start.1 = (f32[4,256,1,256]{3,1,2,0:T(8,128)S(1)}, f32[4,256,1,256]{3,1,2,0:T(8,128)}, u32[]{:S(2)}) copy-start(f32[4,256,1,256]{3,1,2,0:T(8,128)} %all-gather.13.cloned.1.call-done) | copy-start | bytes 3145732
  357.9 0.7 copy-start.35
  382.7 3.8 copy-start.36
  382.7 3.8 copy-start.37
  390.6 2.3 copy-start.9
  434.4 3.0 copy-start.21
  475.2 3.7 copy-start.8
  475.6 3.5 copy-start.7
  477.7 2.7 copy-start.6
  517.9 4.0 copy-start.5
  519.9 3.2 copy-start.4
Sparse Core Ops, SparseCore 0:
  10.3 80.0 all-gather.8
  156.6 26.5 all-gather.10
  195.8 26.5 all-gather.12
  311.7 76.0 all-gather.14
where the time goes:
time: 595 us; the launch traced here: 584 us
  other arithmetic  234 us (39%)
  local copies, waits for them, and re-layouts  132 us (22%)
  matrix products  120 us (20%)
  waiting for transfers between devices  79.6 us (13%)
  between operations  17.7 us (3%)
    dot_general x239, matrix products, mm(): return jnp.dot(a, b, precision=HIGHEST, preferred_element_type=jnp.float32)  120 us
    another operation x24, other arithmetic, factor_diag(): l11 = jnp.tril(lax.linalg.cholesky(s11, symmetrize_input=True))  102 us
    another operation x24, other arithmetic, factor_diag(): lax.linalg.cholesky(diag[:half, :half], symmetrize_input=False)  99.5 us
    unnamed x139, local copies, waits for them, and re-layouts  84.3 us
    all_gather x2, waiting for transfers between devices, separator_tiles(): pieces.append(lax.all_gather(piece, ('row', 'col'), axis=0))  79.5 us
    reduce_sum x16, other arithmetic, lower_inverse(): diag = jnp.sum(lower * eye, axis=1)  12.5 us
  transfers between devices with their start and end apart: 4, of which 1 were waited for; matrix products, arithmetic and copies ran while one was open for 38% of the time, Pallas kernels for 0%

commit v1 on v0

--- a/solution.py
+++ b/solution.py
@@ -10,33 +10,32 @@
     return jnp.dot(a, b, precision=HIGHEST, preferred_element_type=jnp.float32)
 
 
-def separator_tiles(sep_local, n_row, n_col, n_columns, after_first):
+def separator_panels(sep_local, n_row, n_col, n_columns, after_first):
     sep_slots, tile, cslots, _ = sep_local.shape
-    if sep_slots * n_row == n_columns:
+    if sep_slots == 1 and n_row == n_columns:
         pieces = []
         for t in range(cslots):
-            piece = sep_local[:, :, t, :].reshape(sep_slots * tile, tile)
+            piece = sep_local[0, :, t, :]
             if t == 1:
                 piece = piece + after_first(pieces[0])
-            pieces.append(lax.all_gather(piece, ("row", "col"), axis=0))
+            pieces.append(lax.all_gather(piece, ("col", "row"), axis=0))
         if cslots == 1:
             after_first(pieces[0])
 
-        def get(i, j):
-            g = pieces[j // n_col]
-            row = (i // n_row) * tile
-            return g[(i % n_row) * n_col + j % n_col, row:row + tile]
+        def panel(k):
+            base = (k % n_col) * n_row
+            return pieces[k // n_col][base + k:base + n_row].reshape((n_columns - k) * tile, tile)
 
-        return get
+        return panel
     after_first(None)
     g = lax.all_gather(sep_local, "row", axis=1, tiled=True)
     g = g.reshape(sep_slots * n_row * tile, cslots, tile)[: n_columns * tile]
     g = lax.all_gather(g, "col", axis=2)
 
-    def get(i, j):
-        return g[i * tile:(i + 1) * tile, j // n_col, j % n_col, :]
+    def panel(k):
+        return g[k * tile:, k // n_col, k % n_col, :]
 
-    return get
+    return panel
 
 
 def after(value):
@@ -104,14 +103,13 @@
         return after(tail_pieces[-1])
 
     sep_slots = -(-n_columns // n_row)
-    get_tile = separator_tiles(working[:sep_slots], n_row, n_col, n_columns, gather_tail)
+    get_panel = separator_panels(working[:sep_slots], n_row, n_col, n_columns, gather_tail)
 
     total_rows = n_columns * tile + n_tail
     factor = jnp.zeros((total_rows, n_columns * tile), jnp.float32)
     for k in range(n_columns):
         cols = slice(k * tile, (k + 1) * tile)
-        parts = [get_tile(i, k) for i in range(k, n_columns)] + [tail_pieces[k // n_col][k % n_col]]
-        panel = jnp.concatenate(parts, axis=0)
+        panel = jnp.concatenate([get_panel(k), tail_pieces[k // n_col][k % n_col]], axis=0)
         if k > 0:
             left = factor[k * tile:, : k * tile]
             top = factor[k * tile:(k + 1) * tile, : k * tile]

time: 595 us -> 571 us (0.960)
  local copies, waits for them, and re-layouts: 132 us -> 89 us
  waiting for transfers between devices: 79.6 us -> 105 us
    unnamed x139 -> x76, local copies, waits for them, and re-layouts: 84.3 us -> 27.4 us
    all_gather x2, waiting for transfers between devices: 0.02 us -> 25 us  [gather_tail(): tail_pieces.append(lax.all_gather(piece, 'col', axis=0))]
    reshape x0 -> x5, local copies, waits for them, and re-layouts: none -> 8.23 us  [panel(): pieces[k // n_col][base + k:base + n_row]]
    slice x3 -> x9, local copies, waits for them, and re-layouts: 7.8 us -> 15 us  [the longest x8 14.3 us: panel(): pieces[k // n_col][base + k:base + n_row]]
  transfers between devices with their start and end apart: 4 -> 4, of which waited for: 1 -> 2; matrix products, arithmetic and copies ran while one was open for 38% -> 31% of each run, Pallas kernels for 0% -> 0%
where the time goes in v1:
time: 571 us; the launch traced here: 561 us
  other arithmetic  231 us (40%)
  matrix products  118 us (21%)
  waiting for transfers between devices  105 us (18%)
  local copies, waits for them, and re-layouts  89 us (16%)
  between operations  17.6 us (3%)
    dot_general x239, matrix products, mm(): return jnp.dot(a, b, precision=HIGHEST, preferred_element_type=jnp.float32)  118 us
    another operation x24, other arithmetic, factor_diag(): l11 = jnp.tril(lax.linalg.cholesky(s11, symmetrize_input=True))  102 us
    another operation x24, other arithmetic, factor_diag(): lax.linalg.cholesky(diag[:half, :half], symmetrize_input=False)  99.2 us
    all_gather x2, waiting for transfers between devices, separator_panels(): pieces.append(lax.all_gather(piece, ('col', 'row'), axis=0))  79.6 us
    unnamed x76, local copies, waits for them, and re-layouts  27.4 us
    all_gather x2, waiting for transfers between devices, gather_tail(): tail_pieces.append(lax.all_gather(piece, 'col', axis=0))  25 us
    slice x8, local copies, waits for them, and re-layouts, panel(): pieces[k // n_col][base + k:base + n_row]  14.3 us
    reduce_sum x16, other arithmetic, lower_inverse(): diag = jnp.sum(lower * eye, axis=1)  12.1 us
  transfers between devices with their start and end apart: 4, of which 2 were waited for; matrix products, arithmetic and copies ran while one was open for 31% of the time, Pallas kernels for 0%

profile of v1, /device:TPU:0, one launch (start us, length us, event | category | flops | bytes accessed | tf_op | source)
XLA Modules:
  0.0 560.7 jit_solution(4404371159626018793)
XLA Ops:
  11.9 79.6 %all-gather.9.cloned.1.call-done = f32[32,256,1,256]{3,1,2,0:T(8,128)} async-done(((f32[1,256,1,256]{3,1,2,0:T(8,128)}), f32[32,256,1,256]{3,1,2,0:T(8,128)}) %all-gather.9.cloned.1.call-update) | async-done | bytes 8388624 | tf_op jit(solution)/shard_map/all_gather | solution.py:21
  93.7 11.7 %custom-call.18 = f32[128,128]{1,0:T(8,128)S(1)} custom-call(f32[128,128]{1,0:T(8,128)S(1)} %copy.320), custom_call_target="Cholesky" | custom-call | tf_op jit(solution)/shard_map/cholesky/custom-call.1 | solution.py:62
  110.3 11.7 %custom-call.19 = f32[128,128]{1,0:T(8,128)S(1)} custom-call(f32[128,128]{1,0:T(8,128)S(1)} %copy.324), custom_call_target="Cholesky" | custom-call | tf_op jit(solution)/shard_map/cholesky/custom-call.1 | solution.py:66
  127.9 2.8 slice.519
  130.7 2.9 slice.510
  133.6 1.8 slice.505
  138.2 3.1 copy.345
  141.3 3.1 copy.331
  144.4 12.2 %copy.513 = f32[1024,2,8,128]{3,1,2,0:T(2,128)S(1)} copy(f32[1024,2,8,128]{3,2,1,0:T(8,128)} %bitcast.413) | data formatting | bytes 16777216
  160.5 25.0 %all-gather.11.cloned.1.call-done = f32[4,256,1,256]{3,1,2,0:T(8,128)} async-done(((f32[1,256,1,256]{3,1,2,0:T(8,128)}), f32[4,256,1,256]{3,1,2,0:T(8,128)}) %all-gather.11.cloned.1.call-update) | async-done | bytes 1048592 | tf_op jit(solution)/shard_map/all_gather | solution.py:102
  185.5 2.1 fusion.303
  187.6 1.8 copy.456
  189.4 2.8 fusion.26
  193.8 2.0 convolution_subtract_fusion
  197.9 1.8 copy.334
  201.7 11.7 %custom-call.20 = f32[128,128]{1,0:T(8,128)S(1)} custom-call(f32[128,128]{1,0:T(8,128)S(1)} %copy.335), custom_call_target="Cholesky" | custom-call | tf_op jit(solution)/shard_map/cholesky/custom-call.1 | solution.py:62
  223.4 13.3 %custom-call.21 = f32[128,128]{1,0:T(8,128)} custom-call(f32[128,128]{1,0:T(8,128)} %copy.339), custom_call_target="Cholesky" | custom-call | tf_op jit(solution)/shard_map/cholesky/custom-call.1 | solution.py:66
  244.5 1.8 copy.457
  250.8 5.8 %fusion.31 = f32[1792,256]{1,0:T(8,128)} fusion(f32[2048,256]{0,1:T(8,128)} %copy-done, f32[128,128]{1,0:T(8,128)} %copy-done.19, f32[128,128]{1,0:T(8,128)S(1)} %convolution_divide_fusion.12, f32[128,128]{1,0:T(8,128)S(1)} %convolution_negate_fusion.6), kind=kOutput, calls=%fused_computation.145 | convolution fusion | flops 1409548288 | bytes 3866624 | tf_op jit(solution)/shard_map/dot_general | solution.py:10
  256.6 1.8 copy.514
  260.3 9.0 %scatter.26 = f32[2304,2048]{1,0:T(8,128)} pad(f32[2304,256]{1,0:T(8,128)S(1)} %fusion.22, f32[]{:T(128)} %constant.351.clone.1), padding=0_0x0_1792 | pad | bytes 21233668 | tf_op jit(solution)/shard_map/scatter | solution.py:121
  271.5 5.9 %fusion.18 = f32[1792,256]{0,1:T(8,128)S(1)} fusion(f32[2304,2048]{1,0:T(8,128)} %fusion.24, f32[256,256]{0,1:T(8,128)S(1)} %bitcast.431, f32[1536,256]{0,1:T(8,128)S(1)} %copy-done.3), kind=kOutput, calls=%fused_computation.126 | convolution fusion | flops 2819489792 | bytes 7864320 | tf_op jit(solution)/shard_map/dot_general | solution.py:10
  278.5 11.7 %custom-call.22 = f32[128,128]{1,0:T(8,128)S(1)} custom-call(f32[128,128]{1,0:T(8,128)S(1)} %copy.349), custom_call_target="Cholesky" | custom-call | tf_op jit(solution)/shard_map/cholesky/custom-call.1 | solution.py:62
  294.0 1.8 copy.460
  299.9 11.7 %custom-call.23 = f32[128,128]{1,0:T(8,128)S(1)} custom-call(f32[128,128]{1,0:T(8,128)S(1)} %copy.353), custom_call_target="Cholesky" | custom-call | tf_op jit(solution)/shard_map/cholesky/custom-call.1 | solution.py:66
  316.4 2.7 fusion.36
  321.0 6.5 %fusion.15 = f32[1536,256]{0,1:T(8,128)S(1)} fusion(f32[2304,2048]{1,0:T(8,128)} %fusion.30, f32[256,256]{0,1:T(8,128)S(1)} %bitcast.430, f32[1280,256]{0,1:T(8,128)S(1)} %copy-done.4), kind=kOutput, calls=%fused_computation.13 | convolution fusion | flops 3624665088 | bytes 8650752 | tf_op jit(solution)/shard_map/dot_general | solution.py:10
  327.9 11.7 %custom-call.24 = f32[128,128]{1,0:T(8,128)S(1)} custom-call(f32[128,128]{1,0:T(8,128)S(1)} %copy.363), custom_call_target="Cholesky" | custom-call | tf_op jit(solution)/shard_map/cholesky/custom-call.1 | solution.py:62
  344.6 11.7 %custom-call.25 = f32[128,128]{1,0:T(8,128)S(1)} custom-call(f32[128,128]{1,0:T(8,128)S(1)} %copy.367), custom_call_target="Cholesky" | custom-call | tf_op jit(solution)/shard_map/cholesky/custom-call.1 | solution.py:66
  360.9 2.7 fusion.44
  364.9 1.9 slice.558
  369.6 7.5 %fusion.12 = f32[1280,256]{0,1:T(8,128)S(1)} fusion(f32[2304,2048]{1,0:T(8,128)} %fusion.35, f32[256,256]{0,1:T(8,128)} %bitcast.429, f32[1024,256]{0,1:T(8,128)S(1)} %copy.373), kind=kOutput, calls=%fused_computation.12 | convolution fusion | flops 4027187200 | bytes 8912896 | tf_op jit(solution)/shard_map/dot_general | solution.py:10
  377.5 11.7 %custom-call.26 = f32[128,128]{1,0:T(8,128)S(1)} custom-call(f32[128,128]{1,0:T(8,128)S(1)} %copy.377), custom_call_target="Cholesky" | custom-call | tf_op jit(solution)/shard_map/cholesky/custom-call.1 | solution.py:62
  394.1 11.7 %custom-call.27 = f32[128,128]{1,0:T(8,128)S(1)} custom-call(f32[128,128]{1,0:T(8,128)S(1)} %copy.381), custom_call_target="Cholesky" | custom-call | tf_op jit(solution)/shard_map/cholesky/custom-call.1 | solution.py:66
  410.5 1.8 fusion.58
  413.5 6.8 %fusion.38 = f32[1024,256]{1,0:T(8,128)S(1)} fusion(f32[2304,2048]{1,0:T(8,128)} %fusion.43, f32[256,256]{1,0:T(8,128)S(1)} %copy-done.12, f32[768,256]{1,0:T(8,128)S(1)} %bitcast.423), kind=kOutput, calls=%fused_computation.154 | convolution fusion | flops 4027056128 | bytes 8650752 | tf_op jit(solution)/shard_map/dot_general | solution.py:10
  420.7 11.7 %custom-call.28 = f32[128,128]{1,0:T(8,128)S(1)} custom-call(f32[128,128]{1,0:T(8,128)S(1)} %copy.388), custom_call_target="Cholesky" | custom-call | tf_op jit(solution)/shard_map/cholesky/custom-call.1 | solution.py:62
  437.2 11.7 %custom-call.29 = f32[128,128]{1,0:T(8,128)S(1)} custom-call(f32[128,128]{1,0:T(8,128)S(1)} %copy.392), custom_call_target="Cholesky" | custom-call | tf_op jit(solution)/shard_map/cholesky/custom-call.1 | solution.py:66
  456.1 7.1 %fusion.46 = f32[768,256]{0,1:T(8,128)S(1)} fusion(f32[2304,2048]{1,0:T(8,128)} %fusion.57, f32[256,256]{0,1:T(8,128)S(1)} %bitcast.428, f32[512,256]{0,1:T(8,128)S(1)} %copy.398), kind=kOutput, calls=%fused_computation.162 | convolution fusion | flops 3624271872 | bytes 7864320 | tf_op jit(solution)/shard_map/dot_general | solution.py:10
  463.6 11.7 %custom-call.30 = f32[128,128]{1,0:T(8,128)S(1)} custom-call(f32[128,128]{1,0:T(8,128)S(1)} %copy.402), custom_call_target="Cholesky" | custom-call | tf_op jit(solution)/shard_map/cholesky/custom-call.1 | solution.py:62
  480.1 11.9 %custom-call.31 = f32[128,128]{1,0:T(8,128)S(1)} custom-call(f32[128,128]{1,0:T(8,128)S(1)} %fusion.222), custom_call_target="Cholesky" | custom-call | tf_op jit(solution)/shard_map/cholesky/custom-call.1 | solution.py:66
  499.8 5.9 %fusion.51 = f32[512,256]{0,1:T(8,128)S(1)} fusion(f32[2304,2048]{1,0:T(8,128)} %fusion.63, f32[256,256]{0,1:T(8,128)S(1)} %bitcast.427, f32[256,256]{0,1:T(8,128)S(1)} %bitcast.432), kind=kOutput, calls=%fused_computation.163 | convolution fusion | flops 2818834432 | bytes 6553600 | tf_op jit(solution)/shard_map/dot_general | solution.py:10
  506.1 11.9 %custom-call.32 = f32[128,128]{1,0:T(8,128)S(1)} custom-call(f32[128,128]{1,0:T(8,128)S(1)} %copy.413), custom_call_target="Cholesky" | custom-call | tf_op jit(solution)/shard_map/cholesky/custom-call.1 | solution.py:62
  522.8 11.7 %custom-call.33 = f32[128,128]{1,0:T(8,128)S(1)} custom-call(f32[128,128]{1,0:T(8,128)S(1)} %broadcast_multiply_fusion.1), custom_call_target="Cholesky" | custom-call | tf_op jit(solution)/shard_map/cholesky/custom-call.1 | solution.py:66
  540.8 3.9 constant_dynamic-slice_fusion.3
  544.7 2.9 copy.420
  548.9 1.9 copy.422
  552.2 1.8 copy.424
  (462 shorter events, 133.2 us)
Async XLA Ops:
  6.5 84.9 %all-gather.9.cloned.1.call-start = ((), (), s32[]{:S(2)}) async-start(), calls=%async_computation | async-start | bytes 8650752 | tf_op jit(solution)/shard_map/all_gather | solution.py:21
  9.5 1.0 copy-start.5
  11.2 174.3 %all-gather.11.cloned.1.call-start = ((), (), s32[]{:S(2)}) async-start(), calls=%async_computation.1 | async-start | bytes 1310720 | tf_op jit(solution)/shard_map/all_gather | solution.py:102
  106.8 0.6 copy-start.20
  109.6 18.3 %copy-start.18 = (f32[128,128]{1,0:T(8,128)}, f32[128,128]{1,0:T(8,128)S(1)}, u32[]{:S(2)}) copy-start(f32[128,128]{1,0:T(8,128)S(1)} %convolution_divide_fusion.15) | copy-start | bytes 196612
  123.4 7.3 %copy-start.24 = (f32[128,128]{1,0:T(8,128)}, f32[128,128]{1,0:T(8,128)S(1)}, u32[]{:S(2)}) copy-start(f32[128,128]{1,0:T(8,128)S(1)} %get-tuple-element.131) | copy-start | bytes 196612
  133.6 2.1 copy-start.32
  144.4 13.5 %copy-start.6 = (f32[2,256,2,256]{3,1,2,0:T(8,128)S(1)}, f32[2,256,2,256]{3,1,2,0:T(8,128)}, u32[]{:S(2)}) copy-start(f32[2,256,2,256]{3,1,2,0:T(8,128)} %copy-done.5) | copy-start | bytes 3145732
  156.7 2.2 copy-start.31
  156.7 3.5 copy-start.30
  158.8 97.7 %all-gather.13.cloned.1.call-start = ((), (), s32[]{:S(2)}) async-start(), calls=%async_computation.2 | async-start | bytes 1310720 | tf_op jit(solution)/shard_map/all_gather | solution.py:102
  160.4 204.5 %all-gather.15.cloned.1.call-start = ((), (), s32[]{:S(2)}) async-start(), calls=%async_computation.3 | async-start | bytes 8650752 | tf_op jit(solution)/shard_map/all_gather | solution.py:21
  189.4 2.8 copy-start.21
  189.4 2.8 copy-start.25
  189.4 2.9 copy-start.26
  192.2 1.6 copy-start.1
  192.3 1.6 copy-start.11
  195.9 1.4 copy-start
  200.9 0.7 copy-start.16
  213.4 4.2 copy-start.17
  214.8 0.6 copy-start.22
  217.6 24.1 %copy-start.19 = (f32[128,128]{1,0:T(8,128)}, f32[128,128]{1,0:T(8,128)S(1)}, u32[]{:S(2)}) copy-start(f32[128,128]{1,0:T(8,128)S(1)} %convolution_divide_fusion.13) | copy-start | bytes 196612
  239.8 0.8 copy-start.27
  260.2 9.0 %copy-start.2 = (f32[1792,256]{1,0:T(8,128)S(1)}, f32[1792,256]{1,0:T(8,128)}, u32[]{:S(2)}) copy-start(f32[1792,256]{1,0:T(8,128)} %fusion.31) | copy-start | bytes 5505028
  260.3 9.0 %copy-start.23 = (f32[128,128]{1,0:T(8,128)S(1)}, f32[128,128]{1,0:T(8,128)}, u32[]{:S(2)}) copy-start(f32[128,128]{1,0:T(8,128)} %copy-done.22) | copy-start | bytes 196612
  260.3 9.0 %copy-start.28 = (f32[128,128]{1,0:T(8,128)S(1)}, f32[128,128]{1,0:T(8,128)}, u32[]{:S(2)}) copy-start(f32[128,128]{1,0:T(8,128)} %copy-done.27) | copy-start | bytes 196612
  260.3 9.0 %copy-start.29 = (f32[128,128]{1,0:T(8,128)S(1)}, f32[128,128]{1,0:T(8,128)}, u32[]{:S(2)}) copy-start(f32[128,128]{1,0:T(8,128)} %copy.340) | copy-start | bytes 196612
  269.3 2.2 copy-start.3
  269.3 2.2 copy-start.10
  277.4 14.1 %copy-start.7 = (f32[4,256,1,256]{3,1,2,0:T(8,128)S(1)}, f32[4,256,1,256]{3,1,2,0:T(8,128)}, u32[]{:S(2)}) copy-start(f32[4,256,1,256]{3,1,2,0:T(8,128)} %all-gather.13.cloned.1.call-done) | copy-start | bytes 3145732
  277.6 15.2 %copy-start.13 = (f32[1,256,1,256]{3,1,2,0:T(8,128)S(1)}, f32[1,256,1,256]{3,1,2,0:T(8,128)}, u32[]{:S(2)}) copy-start(f32[1,256,1,256]{3,1,2,0:T(8,128)} %get-tuple-element.140) | copy-start | bytes 786436
  277.7 0.7 copy-start.14
  292.9 6.2 %copy-start.15 = (f32[256,256]{0,1:T(8,128)S(1)}, f32[256,256]{0,1:T(8,128)}, u32[]{:S(2)}) copy-start(f32[256,256]{0,1:T(8,128)} %copy-done.14) | copy-start | bytes 786436
  319.1 1.9 copy-start.4
  410.5 3.0 copy-start.12
  434.5 16.8 %copy-start.8 = (f32[2,256,1,256]{3,1,0,2:T(8,128)S(1)}, f32[2,256,1,256]{3,1,0,2:T(8,128)}, u32[]{:S(2)}) copy-start(f32[2,256,1,256]{3,1,0,2:T(8,128)} %slice.558) | copy-start | bytes 1572868
  453.3 2.8 copy-start.9
Sparse Core Ops, SparseCore 0:
  11.3 80.1 all-gather.8
  159.0 26.5 all-gather.10
  187.1 27.4 all-gather.12
  260.4 77.1 all-gather.14

commit v2 on v1

--- a/solution.py
+++ b/solution.py
@@ -6,8 +6,8 @@
 HIGHEST = lax.Precision.HIGHEST
 
 
-def mm(a, b):
-    return jnp.dot(a, b, precision=HIGHEST, preferred_element_type=jnp.float32)
+def mm(a, b, precision=HIGHEST):
+    return jnp.dot(a, b, precision=precision, preferred_element_type=jnp.float32)
 
 
 def separator_panels(sep_local, n_row, n_col, n_columns, after_first):
@@ -92,11 +92,13 @@
     tail_first = n_columns // n_row
     n_tail = (slot_count - tail_first) * tile
     tail_pieces = []
+    tail_sources = []
 
     def gather_tail(first_piece):
         tail_local = working[tail_first:]
         if first_piece is not None:
             tail_local = tail_local + after(first_piece)
+        tail_sources.append(tail_local)
         for t in range(col_slot_count):
             piece = tail_local[:, :, t, :].reshape(n_tail, tile)
             tail_pieces.append(lax.all_gather(piece, "col", axis=0))
@@ -113,8 +115,10 @@
         if k > 0:
             left = factor[k * tile:, : k * tile]
             top = factor[k * tile:(k + 1) * tile, : k * tile]
-            panel = panel - mm(left, top.T)
+            panel = panel - mm(left, top.T, lax.Precision.HIGH)
         diag = panel[:tile]
+        if k == 0:
+            diag = diag + after(tail_sources[0])
         diag = jnp.tril(diag) + jnp.tril(diag, -1).T
         lkk, linv = factor_diag(diag)
         below = mm(panel[tile:], linv.T)

time: 571 us -> 544 us (0.953)
  matrix products: 118 us -> 98.3 us
  local copies, waits for them, and re-layouts: 89 us -> 80.1 us
    dot_general x239, matrix products: 118 us -> 98.3 us  [mm(): jnp.dot(a, b, precision=precision, preferred_element_type=jnp.float32)]
    unnamed x76 -> x63, local copies, waits for them, and re-layouts: 27.4 us -> 20.3 us
  transfers between devices with their start and end apart: 4 -> 4, of which waited for: 2 -> 2; matrix products, arithmetic and copies ran while one was open for 31% -> 28% of each run, Pallas kernels for 0% -> 0%
where the time goes in v2:
time: 544 us; the launch traced here: 533 us
  other arithmetic  233 us (43%)
  waiting for transfers between devices  104 us (19%)
  matrix products  98.3 us (18%)
  local copies, waits for them, and re-layouts  80.1 us (15%)
  between operations  18.5 us (3%)
    another operation x24, other arithmetic, factor_diag(): l11 = jnp.tril(lax.linalg.cholesky(s11, symmetrize_input=True))  100 us
    another operation x24, other arithmetic, factor_diag(): lax.linalg.cholesky(diag[:half, :half], symmetrize_input=False)  99.7 us
    dot_general x239, matrix products, mm(): jnp.dot(a, b, precision=precision, preferred_element_type=jnp.float32)  98.3 us
    all_gather x2, waiting for transfers between devices, separator_panels(): pieces.append(lax.all_gather(piece, ('col', 'row'), axis=0))  79.5 us
    all_gather x2, waiting for transfers between devices, gather_tail(): tail_pieces.append(lax.all_gather(piece, 'col', axis=0))  24.4 us
    unnamed x63, local copies, waits for them, and re-layouts  20.3 us
    slice x8, local copies, waits for them, and re-layouts, panel(): pieces[k // n_col][base + k:base + n_row]  13 us
    reduce_sum x16, other arithmetic, lower_inverse(): diag = jnp.sum(lower * eye, axis=1)  11.4 us
  transfers between devices with their start and end apart: 4, of which 2 were waited for; matrix products, arithmetic and copies ran while one was open for 28% of the time, Pallas kernels for 0%

profile of v2, /device:TPU:0, one launch (start us, length us, event | category | flops | bytes accessed | tf_op | source)
XLA Modules:
  0.0 533.4 jit_solution(12927652209826464695)
XLA Ops:
  11.9 79.5 %all-gather.9.cloned.1.call-done = f32[32,256,1,256]{3,1,2,0:T(8,128)} async-done(((f32[1,256,1,256]{3,1,2,0:T(8,128)}), f32[32,256,1,256]{3,1,2,0:T(8,128)}) %all-gather.9.cloned.1.call-update) | async-done | bytes 8388624 | tf_op jit(solution)/shard_map/all_gather | solution.py:21
  93.0 3.0 slice.521
  96.0 3.0 slice.512
  99.2 4.9 copy.516
  108.2 1.8 copy.459
  112.5 1.7 add_bitcast_fusion
  114.2 1.8 copy.323
  117.9 11.7 %custom-call.18 = f32[128,128]{1,0:T(8,128)S(1)} custom-call(f32[128,128]{1,0:T(8,128)S(1)} %copy.324), custom_call_target="Cholesky" | custom-call | tf_op jit(solution)/shard_map/cholesky/custom-call.1 | solution.py:62
  138.7 12.5 %custom-call.19 = f32[128,128]{1,0:T(8,128)S(1)} custom-call(f32[128,128]{1,0:T(8,128)} %copy.328), custom_call_target="Cholesky" | custom-call | tf_op jit(solution)/shard_map/cholesky/custom-call.1 | solution.py:66
  154.3 1.7 fusion.311
  158.2 3.5 copy.349
  161.7 2.8 copy.335
  166.8 24.4 %all-gather.11.cloned.1.call-done = f32[4,256,1,256]{3,1,2,0:T(8,128)} async-done(((f32[1,256,1,256]{3,1,2,0:T(8,128)}), f32[4,256,1,256]{3,1,2,0:T(8,128)}) %all-gather.11.cloned.1.call-update) | async-done | bytes 1048592 | tf_op jit(solution)/shard_map/all_gather | solution.py:104
  191.2 2.0 fusion.301
  193.4 1.9 fusion.26
  200.6 11.7 %custom-call.20 = f32[128,128]{1,0:T(8,128)S(1)} custom-call(f32[128,128]{1,0:T(8,128)S(1)} %copy.339), custom_call_target="Cholesky" | custom-call | tf_op jit(solution)/shard_map/cholesky/custom-call.1 | solution.py:62
  217.2 11.9 %custom-call.21 = f32[128,128]{1,0:T(8,128)S(1)} custom-call(f32[128,128]{1,0:T(8,128)S(1)} %copy.343), custom_call_target="Cholesky" | custom-call | tf_op jit(solution)/shard_map/cholesky/custom-call.1 | solution.py:66
  233.9 5.8 %fusion.31 = f32[1792,256]{1,0:T(8,128)} fusion(f32[2048,256]{0,1:T(8,128)} %copy-done.1, f32[128,128]{1,0:T(8,128)S(1)} %convolution_divide_fusion.13, f32[128,128]{1,0:T(8,128)S(1)} %convolution_divide_fusion.12, f32[128,128]{1,0:T(8,128)S(1)} %convolution_negate_fusion.6), kind=kOutput, calls=%fused_computation.145 | convolution fusion | flops 1409548288 | bytes 3866624 | tf_op jit(solution)/shard_map/dot_general | solution.py:10
  239.6 1.8 copy.518
  242.7 1.7 slice_add_fusion.1
  244.4 9.0 %scatter.26 = f32[2304,2048]{1,0:T(8,128)} pad(f32[2304,256]{1,0:T(8,128)S(1)} %fusion.22, f32[]{:T(128)} %constant.352.clone.1), padding=0_0x0_1792 | pad | bytes 21233668 | tf_op jit(solution)/shard_map/scatter | solution.py:125
  255.6 3.8 fusion.18
  260.5 11.9 %custom-call.22 = f32[128,128]{1,0:T(8,128)S(1)} custom-call(f32[128,128]{1,0:T(8,128)S(1)} %copy.353), custom_call_target="Cholesky" | custom-call | tf_op jit(solution)/shard_map/cholesky/custom-call.1 | solution.py:62
  276.2 1.8 copy.464
  282.0 11.7 %custom-call.23 = f32[128,128]{1,0:T(8,128)S(1)} custom-call(f32[128,128]{1,0:T(8,128)S(1)} %copy.357), custom_call_target="Cholesky" | custom-call | tf_op jit(solution)/shard_map/cholesky/custom-call.1 | solution.py:66
  298.4 3.1 fusion.36
  303.4 4.7 fusion.15
  308.5 11.7 %custom-call.24 = f32[128,128]{1,0:T(8,128)S(1)} custom-call(f32[128,128]{1,0:T(8,128)S(1)} %copy.367), custom_call_target="Cholesky" | custom-call | tf_op jit(solution)/shard_map/cholesky/custom-call.1 | solution.py:62
  325.2 11.8 %custom-call.25 = f32[128,128]{1,0:T(8,128)S(1)} custom-call(f32[128,128]{1,0:T(8,128)S(1)} %copy.371), custom_call_target="Cholesky" | custom-call | tf_op jit(solution)/shard_map/cholesky/custom-call.1 | solution.py:66
  341.6 2.3 fusion.44
  345.2 1.9 slice.560
  349.9 5.0 fusion.12
  355.4 11.7 %custom-call.26 = f32[128,128]{1,0:T(8,128)S(1)} custom-call(f32[128,128]{1,0:T(8,128)S(1)} %copy.381), custom_call_target="Cholesky" | custom-call | tf_op jit(solution)/shard_map/cholesky/custom-call.1 | solution.py:62
  372.0 11.7 %custom-call.27 = f32[128,128]{1,0:T(8,128)S(1)} custom-call(f32[128,128]{1,0:T(8,128)S(1)} %copy.385), custom_call_target="Cholesky" | custom-call | tf_op jit(solution)/shard_map/cholesky/custom-call.1 | solution.py:66
  388.4 1.8 fusion.58
  391.4 5.1 fusion.38
  396.9 12.1 %custom-call.28 = f32[128,128]{1,0:T(8,128)S(1)} custom-call(f32[128,128]{1,0:T(8,128)S(1)} %copy.392), custom_call_target="Cholesky" | custom-call | tf_op jit(solution)/shard_map/cholesky/custom-call.1 | solution.py:62
  413.7 11.7 %custom-call.29 = f32[128,128]{1,0:T(8,128)S(1)} custom-call(f32[128,128]{1,0:T(8,128)S(1)} %copy.396), custom_call_target="Cholesky" | custom-call | tf_op jit(solution)/shard_map/cholesky/custom-call.1 | solution.py:66
  432.2 5.1 fusion.46
  437.7 11.7 %custom-call.30 = f32[128,128]{1,0:T(8,128)S(1)} custom-call(f32[128,128]{1,0:T(8,128)S(1)} %copy.406), custom_call_target="Cholesky" | custom-call | tf_op jit(solution)/shard_map/cholesky/custom-call.1 | solution.py:62
  454.1 11.7 %custom-call.31 = f32[128,128]{1,0:T(8,128)S(1)} custom-call(f32[128,128]{1,0:T(8,128)S(1)} %fusion.220), custom_call_target="Cholesky" | custom-call | tf_op jit(solution)/shard_map/cholesky/custom-call.1 | solution.py:66
  473.9 4.2 fusion.51
  478.5 11.7 %custom-call.32 = f32[128,128]{1,0:T(8,128)S(1)} custom-call(f32[128,128]{1,0:T(8,128)S(1)} %copy.417), custom_call_target="Cholesky" | custom-call | tf_op jit(solution)/shard_map/cholesky/custom-call.1 | solution.py:62
  495.1 11.9 %custom-call.33 = f32[128,128]{1,0:T(8,128)S(1)} custom-call(f32[128,128]{1,0:T(8,128)S(1)} %broadcast_multiply_fusion.1), custom_call_target="Cholesky" | custom-call | tf_op jit(solution)/shard_map/cholesky/custom-call.1 | solution.py:66
  513.3 3.9 constant_dynamic-slice_fusion.3
  517.2 2.9 copy.424
  521.5 1.9 copy.426
  524.7 1.8 copy.428
  (453 shorter events, 126.2 us)
Async XLA Ops:
  6.5 84.9 %all-gather.9.cloned.1.call-start = ((), (), s32[]{:S(2)}) async-start(), calls=%async_computation | async-start | bytes 8650752 | tf_op jit(solution)/shard_map/all_gather | solution.py:21
  9.5 1.0 copy-start.6
  11.2 180.0 %all-gather.11.cloned.1.call-start = ((), (), s32[]{:S(2)}) async-start(), calls=%async_computation.1 | async-start | bytes 1310720 | tf_op jit(solution)/shard_map/all_gather | solution.py:104
  91.5 7.6 %copy-start = (f32[32,256,1,256]{3,1,2,0:T(8,128)S(1)}, f32[32,256,1,256]{3,1,2,0:T(8,128)}, u32[]{:S(2)}) copy-start(f32[32,256,1,256]{3,1,2,0:T(8,128)} %all-gather.9.cloned.1.call-done) | copy-start | bytes 25165828
  99.2 6.2 %copy-start.7 = (f32[2,256,2,256]{3,1,2,0:T(8,128)S(1)}, f32[2,256,2,256]{3,1,2,0:T(8,128)}, u32[]{:S(2)}) copy-start(f32[2,256,2,256]{3,1,2,0:T(8,128)} %copy-done.6) | copy-start | bytes 3145732
  117.1 0.7 copy-start.15
  129.6 4.9 copy-start.16
  131.0 0.6 copy-start.19
  133.9 0.6 copy-start.17
  152.8 0.6 copy-start.21
  161.7 3.1 copy-start.25
  161.7 4.9 copy-start.24
  164.5 75.1 %all-gather.13.cloned.1.call-start = ((), (), s32[]{:S(2)}) async-start(), calls=%async_computation.2 | async-start | bytes 1310720 | tf_op jit(solution)/shard_map/all_gather | solution.py:104
  165.2 28.1 %copy-start.18 = (f32[128,128]{1,0:T(8,128)S(1)}, f32[128,128]{1,0:T(8,128)}, u32[]{:S(2)}) copy-start(f32[128,128]{1,0:T(8,128)} %copy-done.17) | copy-start | bytes 196612
  166.3 178.9 %all-gather.15.cloned.1.call-start = ((), (), s32[]{:S(2)}) async-start(), calls=%async_computation.3 | async-start | bytes 8650752 | tf_op jit(solution)/shard_map/all_gather | solution.py:21
  193.4 2.0 copy-start.20
  193.4 2.0 copy-start.22
  193.4 2.0 copy-start.23
  195.4 1.5 copy-start.2
  197.9 1.4 copy-start.1
  244.4 9.0 %copy-start.3 = (f32[1792,256]{1,0:T(8,128)S(1)}, f32[1792,256]{1,0:T(8,128)}, u32[]{:S(2)}) copy-start(f32[1792,256]{1,0:T(8,128)} %fusion.31) | copy-start | bytes 5505028
  253.4 2.2 copy-start.4
  259.4 14.3 %copy-start.8 = (f32[4,256,1,256]{3,1,2,0:T(8,128)S(1)}, f32[4,256,1,256]{3,1,2,0:T(8,128)}, u32[]{:S(2)}) copy-start(f32[4,256,1,256]{3,1,2,0:T(8,128)} %all-gather.13.cloned.1.call-done) | copy-start | bytes 3145732
  259.5 15.4 %copy-start.12 = (f32[1,256,1,256]{3,1,2,0:T(8,128)S(1)}, f32[1,256,1,256]{3,1,2,0:T(8,128)}, u32[]{:S(2)}) copy-start(f32[1,256,1,256]{3,1,2,0:T(8,128)} %get-tuple-element.140) | copy-start | bytes 786436
  259.6 0.7 copy-start.13
  275.0 6.2 %copy-start.14 = (f32[256,256]{0,1:T(8,128)S(1)}, f32[256,256]{0,1:T(8,128)}, u32[]{:S(2)}) copy-start(f32[256,256]{0,1:T(8,128)} %copy-done.13) | copy-start | bytes 786436
  301.5 1.9 copy-start.5
  388.4 3.0 copy-start.11
  411.1 16.8 %copy-start.9 = (f32[2,256,1,256]{3,1,0,2:T(8,128)S(1)}, f32[2,256,1,256]{3,1,0,2:T(8,128)}, u32[]{:S(2)}) copy-start(f32[2,256,1,256]{3,1,0,2:T(8,128)} %slice.560) | copy-start | bytes 1572868
  429.8 2.4 copy-start.10
Sparse Core Ops, SparseCore 0:
  11.3 80.1 all-gather.8
  164.7 26.5 all-gather.10
  192.8 27.4 all-gather.12
  244.5 77.2 all-gather.14

commit v3 on v2

--- a/solution.py
+++ b/solution.py
@@ -92,13 +92,11 @@
     tail_first = n_columns // n_row
     n_tail = (slot_count - tail_first) * tile
     tail_pieces = []
-    tail_sources = []
 
     def gather_tail(first_piece):
         tail_local = working[tail_first:]
         if first_piece is not None:
             tail_local = tail_local + after(first_piece)
-        tail_sources.append(tail_local)
         for t in range(col_slot_count):
             piece = tail_local[:, :, t, :].reshape(n_tail, tile)
             tail_pieces.append(lax.all_gather(piece, "col", axis=0))
@@ -107,32 +105,33 @@
     sep_slots = -(-n_columns // n_row)
     get_panel = separator_panels(working[:sep_slots], n_row, n_col, n_columns, gather_tail)
 
-    total_rows = n_columns * tile + n_tail
-    factor = jnp.zeros((total_rows, n_columns * tile), jnp.float32)
+    sep_factor = jnp.zeros((n_columns * tile, n_columns * tile), jnp.float32)
+    tail_factor = jnp.zeros((n_tail, n_columns * tile), jnp.float32)
     for k in range(n_columns):
-        cols = slice(k * tile, (k + 1) * tile)
-        panel = jnp.concatenate([get_panel(k), tail_pieces[k // n_col][k % n_col]], axis=0)
+        panel = get_panel(k)
+        tail_panel = tail_pieces[k // n_col][k % n_col]
         if k > 0:
-            left = factor[k * tile:, : k * tile]
-            top = factor[k * tile:(k + 1) * tile, : k * tile]
-            panel = panel - mm(left, top.T, lax.Precision.HIGH)
+            top = sep_factor[k * tile:(k + 1) * tile, : k * tile]
+            panel = panel - mm(sep_factor[k * tile:, : k * tile], top.T, lax.Precision.HIGH)
+            tail_panel = tail_panel - mm(tail_factor[:, : k * tile], top.T, lax.Precision.HIGH)
         diag = panel[:tile]
-        if k == 0:
-            diag = diag + after(tail_sources[0])
         diag = jnp.tril(diag) + jnp.tril(diag, -1).T
         lkk, linv = factor_diag(diag)
-        below = mm(panel[tile:], linv.T)
-        factor = factor.at[k * tile:, cols].set(jnp.concatenate([lkk, below], axis=0))
+        if k + 1 < n_columns:
+            block = jnp.concatenate([lkk, mm(panel[tile:], linv.T)], axis=0)
+        else:
+            block = lkk
+        sep_factor = lax.dynamic_update_slice(sep_factor, block, (k * tile, k * tile))
+        tail_factor = lax.dynamic_update_slice(tail_factor, mm(tail_panel, linv.T), (0, k * tile))
 
     outs = []
     for slot in range(slot_count):
         tile_row = slot * n_row + row_at
-        if slot < tail_first:
-            start = tile_row * tile
-        else:
-            tail_start = n_columns * tile + (slot - tail_first) * tile
-            start = jnp.where(tile_row < n_columns, tile_row * tile, tail_start)
-        picked = lax.dynamic_slice_in_dim(factor, start, tile, axis=0)
+        start = jnp.minimum(tile_row, n_columns - 1) * tile
+        picked = lax.dynamic_slice_in_dim(sep_factor, start, tile, axis=0)
+        if slot >= tail_first:
+            tail_rows = tail_factor[(slot - tail_first) * tile:(slot - tail_first + 1) * tile]
+            picked = jnp.where(tile_row < n_columns, picked, tail_rows)
         picked = picked.reshape(tile, col_slot_count, n_col, tile)
         picked = lax.dynamic_index_in_dim(picked, col_at, axis=2, keepdims=False)
         outs.append(picked)

time: 544 us -> 592 us (1.088)
  matrix products: 98.3 us -> 131 us
  waiting for transfers between devices: 104 us -> 86.7 us
  local copies, waits for them, and re-layouts: 80.1 us -> 96 us
  other arithmetic: 233 us -> 248 us
    dot_general x239 -> x253, matrix products: 98.3 us -> 131 us  [mm(): jnp.dot(a, b, precision=precision, preferred_element_type=jnp.float32)]
    all_gather x2, waiting for transfers between devices: 24.4 us -> 0.02 us  [gather_tail(): tail_pieces.append(lax.all_gather(piece, 'col', axis=0))]
    unnamed x63 -> x164, local copies, waits for them, and re-layouts: 20.3 us -> 32.8 us
    scatter x1 -> x0, local copies, waits for them, and re-layouts: 8.98 us -> none  [shards(): factor.at[k * tile:, cols].set(jnp.concatenate([lkk, below], axis=0))]
    scatter x7 -> x0, other arithmetic: 8.6 us -> none  [shards(): factor.at[k * tile:, cols].set(jnp.concatenate([lkk, below], axis=0))]
    dynamic_update_slice x0 -> x7, other arithmetic: none -> 8.07 us  [shards(): lax.dynamic_update_slice(sep_factor, block, (k * tile, k * tile))]
    all_gather x2, waiting for transfers between devices: 79.5 us -> 86.6 us  [separator_panels(): pieces.append(lax.all_gather(piece, ('col', 'row'), axis=0))]
    slice x15 -> x13, local copies, waits for them, and re-layouts: 1.76 us -> 8.24 us  [shards(): diag = panel[:tile]]
  transfers between devices with their start and end apart: 4 -> 4, of which waited for: 2 -> 2; matrix products, arithmetic and copies ran while one was open for 28% -> 21% of each run, Pallas kernels for 0% -> 0%
where the time goes in v3:
time: 592 us; the launch traced here: 580 us
  other arithmetic  248 us (42%)
  matrix products  131 us (22%)
  local copies, waits for them, and re-layouts  96 us (16%)
  waiting for transfers between devices  86.7 us (15%)
  between operations  18 us (3%)
    dot_general x253, matrix products, mm(): jnp.dot(a, b, precision=precision, preferred_element_type=jnp.float32)  131 us
    another operation x24, other arithmetic, factor_diag(): l11 = jnp.tril(lax.linalg.cholesky(s11, symmetrize_input=True))  105 us
    another operation x24, other arithmetic, factor_diag(): lax.linalg.cholesky(diag[:half, :half], symmetrize_input=False)  100 us
    all_gather x2, waiting for transfers between devices, separator_panels(): pieces.append(lax.all_gather(piece, ('col', 'row'), axis=0))  86.6 us
    unnamed x164, local copies, waits for them, and re-layouts  32.8 us
    reduce_sum x16, other arithmetic, lower_inverse(): diag = jnp.sum(lower * eye, axis=1)  14.1 us
    slice x7, local copies, waits for them, and re-layouts, panel(): pieces[k // n_col][base + k:base + n_row]  13.9 us
  transfers between devices with their start and end apart: 4, of which 2 were waited for; matrix products, arithmetic and copies ran while one was open for 21% of the time, Pallas kernels for 0%

profile of v3, /device:TPU:0, one launch (start us, length us, event | category | flops | bytes accessed | tf_op | source)
XLA Modules:
  0.0 580.3 jit_solution(1677665077479904780)
XLA Ops:
  11.2 80.2 %all-gather.9.cloned.1.call-done = f32[32,256,1,256]{3,1,2,0:T(8,128)} async-done(((f32[1,256,1,256]{3,1,2,0:T(8,128)}), f32[32,256,1,256]{3,1,2,0:T(8,128)}) %all-gather.9.cloned.1.call-update) | async-done | bytes 8388624 | tf_op jit(solution)/shard_map/all_gather | solution.py:21
  93.7 11.7 %custom-call.18 = f32[128,128]{1,0:T(8,128)S(1)} custom-call(f32[128,128]{1,0:T(8,128)S(1)} %copy.236), custom_call_target="Cholesky" | custom-call | tf_op jit(solution)/shard_map/cholesky/custom-call.1 | solution.py:62
  110.5 11.7 %custom-call.19 = f32[128,128]{1,0:T(8,128)S(1)} custom-call(f32[128,128]{1,0:T(8,128)S(1)} %copy.240), custom_call_target="Cholesky" | custom-call | tf_op jit(solution)/shard_map/cholesky/custom-call.1 | solution.py:66
  128.2 3.7 fusion.332
  134.9 2.1 copy.246
  139.9 3.1 fusion.104
  146.1 1.8 copy.249
  150.4 12.5 %custom-call.20 = f32[128,128]{1,0:T(8,128)S(1)} custom-call(f32[128,128]{1,0:T(8,128)} %copy.250), custom_call_target="Cholesky" | custom-call | tf_op jit(solution)/shard_map/cholesky/custom-call.1 | solution.py:62
  174.9 13.3 %custom-call.21 = f32[128,128]{1,0:T(8,128)} custom-call(f32[128,128]{1,0:T(8,128)} %copy.254), custom_call_target="Cholesky" | custom-call | tf_op jit(solution)/shard_map/cholesky/custom-call.1 | solution.py:66
  201.3 4.7 fusion.28
  207.6 12.2 %copy.432 = f32[1024,2,8,128]{3,1,2,0:T(2,128)S(1)} copy(f32[1024,2,8,128]{3,2,1,0:T(8,128)} %bitcast.444) | data formatting | bytes 16777216
  222.1 2.2 dynamic_update_slice.48
  224.3 1.8 fusion.20
  226.1 5.8 %copy-done = f32[2048,2048]{1,0:T(8,128)} copy-done((f32[2048,2048]{1,0:T(8,128)}, f32[2048,2048]{1,0:T(8,128)S(1)}, u32[]{:S(2)}) %copy-start) | copy-done | bytes 16777240
  233.8 11.7 %custom-call.22 = f32[128,128]{1,0:T(8,128)S(1)} custom-call(f32[128,128]{1,0:T(8,128)S(1)} %copy.263), custom_call_target="Cholesky" | custom-call | tf_op jit(solution)/shard_map/cholesky/custom-call.1 | solution.py:62
  254.5 2.5 slice.372
  257.0 2.8 copy.272
  261.0 11.7 %custom-call.23 = f32[128,128]{1,0:T(8,128)S(1)} custom-call(f32[128,128]{1,0:T(8,128)S(1)} %copy.267), custom_call_target="Cholesky" | custom-call | tf_op jit(solution)/shard_map/cholesky/custom-call.1 | solution.py:66
  277.4 3.4 fusion.39
  285.5 2.4 convolution_subtract_fusion.3
  289.2 4.1 fusion.10
  297.7 11.7 %custom-call.24 = f32[128,128]{1,0:T(8,128)S(1)} custom-call(f32[128,128]{1,0:T(8,128)S(1)} %copy.276), custom_call_target="Cholesky" | custom-call | tf_op jit(solution)/shard_map/cholesky/custom-call.1 | solution.py:62
  322.4 13.2 %custom-call.25 = f32[128,128]{1,0:T(8,128)} custom-call(f32[128,128]{1,0:T(8,128)} %copy.280), custom_call_target="Cholesky" | custom-call | tf_op jit(solution)/shard_map/cholesky/custom-call.1 | solution.py:66
  345.6 1.8 fusion.72
  348.7 2.6 convolution_subtract_fusion.4
  351.3 6.3 %all-gather.13.cloned.1.call-done = f32[32,256,1,256]{3,1,2,0:T(8,128)} async-done(((f32[1,256,1,256]{3,1,2,0:T(8,128)}), f32[32,256,1,256]{3,1,2,0:T(8,128)}) %all-gather.13.cloned.1.call-update) | async-done | bytes 8388624 | tf_op jit(solution)/shard_map/all_gather | solution.py:21
  357.6 1.9 slice.401
  359.5 2.1 slice.393
  364.2 4.6 fusion.32
  371.6 11.7 %custom-call.26 = f32[128,128]{1,0:T(8,128)S(1)} custom-call(f32[128,128]{1,0:T(8,128)S(1)} %copy.289), custom_call_target="Cholesky" | custom-call | tf_op jit(solution)/shard_map/cholesky/custom-call.1 | solution.py:62
  390.8 11.7 %custom-call.27 = f32[128,128]{1,0:T(8,128)S(1)} custom-call(f32[128,128]{1,0:T(8,128)S(1)} %copy.293), custom_call_target="Cholesky" | custom-call | tf_op jit(solution)/shard_map/cholesky/custom-call.1 | solution.py:66
  411.7 4.2 fusion.41
  417.1 11.9 %custom-call.28 = f32[128,128]{1,0:T(8,128)S(1)} custom-call(f32[128,128]{1,0:T(8,128)S(1)} %copy.300), custom_call_target="Cholesky" | custom-call | tf_op jit(solution)/shard_map/cholesky/custom-call.1 | solution.py:62
  438.2 12.5 %custom-call.29 = f32[128,128]{1,0:T(8,128)S(1)} custom-call(f32[128,128]{1,0:T(8,128)} %copy.304), custom_call_target="Cholesky" | custom-call | tf_op jit(solution)/shard_map/cholesky/custom-call.1 | solution.py:66
  461.6 2.2 fusion.51
  465.3 3.8 fusion.44
  469.5 11.7 %custom-call.30 = f32[128,128]{1,0:T(8,128)S(1)} custom-call(f32[128,128]{1,0:T(8,128)S(1)} %copy.313), custom_call_target="Cholesky" | custom-call | tf_op jit(solution)/shard_map/cholesky/custom-call.1 | solution.py:62
  486.1 11.7 %custom-call.31 = f32[128,128]{1,0:T(8,128)S(1)} custom-call(f32[128,128]{1,0:T(8,128)S(1)} %fusion.231), custom_call_target="Cholesky" | custom-call | tf_op jit(solution)/shard_map/cholesky/custom-call.1 | solution.py:66
  509.9 2.3 fusion.64
  513.6 3.0 fusion.56
  519.3 11.7 %custom-call.32 = f32[128,128]{1,0:T(8,128)S(1)} custom-call(f32[128,128]{1,0:T(8,128)S(1)} %copy.323), custom_call_target="Cholesky" | custom-call | tf_op jit(solution)/shard_map/cholesky/custom-call.1 | solution.py:62
  536.5 11.9 %custom-call.33 = f32[128,128]{1,0:T(8,128)S(1)} custom-call(f32[128,128]{1,0:T(8,128)S(1)} %broadcast_multiply_fusion.1), custom_call_target="Cholesky" | custom-call | tf_op jit(solution)/shard_map/cholesky/custom-call.1 | solution.py:66
  553.8 2.5 fusion.59
  557.7 4.8 constant_dynamic-slice_fusion.2
  562.5 2.9 copy.328
  567.2 2.5 reshape.190
  569.6 2.0 constant_dynamic-slice_fusion
  571.8 1.8 copy.341
  (561 shorter events, 185.6 us)
Async XLA Ops:
  6.5 84.9 %all-gather.9.cloned.1.call-start = ((), (), s32[]{:S(2)}) async-start(), calls=%async_computation | async-start | bytes 8650752 | tf_op jit(solution)/shard_map/all_gather | solution.py:21
  11.2 238.4 %all-gather.11.cloned.1.call-start = ((), (), s32[]{:S(2)}) async-start(), calls=%async_computation.1 | async-start | bytes 1310720 | tf_op jit(solution)/shard_map/all_gather | solution.py:102
  123.7 3.0 copy-start.53
  128.2 3.9 copy-start.79
  137.0 6.1 %copy-start.6 = (f32[1792,256]{0,1:T(8,128)S(1)}, f32[1792,256]{0,1:T(8,128)}, u32[]{:S(2)}) copy-start(f32[1792,256]{0,1:T(8,128)} %copy.246) | copy-start | bytes 5505028
  138.2 5.8 copy-start.41
  143.1 63.0 %copy-start.1 = (f32[1792,256]{1,0:T(8,128)}, f32[1792,256]{1,0:T(8,128)S(1)}, u32[]{:S(2)}) copy-start(f32[1792,256]{1,0:T(8,128)S(1)} %fusion.104) | copy-start | bytes 5505028
  163.0 6.2 %copy-start.36 = (f32[256,256]{0,1:T(8,128)S(1)}, f32[256,256]{0,1:T(8,128)}, u32[]{:S(2)}) copy-start(f32[256,256]{0,1:T(8,128)} %copy-done.35) | copy-start | bytes 786436
  197.4 4.0 copy-start.3
  199.6 6.4 %copy-start.52 = (f32[128,128]{1,0:T(8,128)S(1)}, f32[128,128]{1,0:T(8,128)}, u32[]{:S(2)}) copy-start(f32[128,128]{1,0:T(8,128)} %copy-done.51) | copy-start | bytes 196612
  199.6 6.4 %copy-start.54 = (f32[128,128]{1,0:T(8,128)S(1)}, f32[128,128]{1,0:T(8,128)}, u32[]{:S(2)}) copy-start(f32[128,128]{1,0:T(8,128)} %copy-done.53) | copy-start | bytes 196612
  199.6 6.4 %copy-start.55 = (f32[128,128]{1,0:T(8,128)S(1)}, f32[128,128]{1,0:T(8,128)}, u32[]{:S(2)}) copy-start(f32[128,128]{1,0:T(8,128)} %copy.241) | copy-start | bytes 196612
  207.5 13.5 %copy-start.12 = (f32[2,256,2,256]{3,1,2,0:T(8,128)S(1)}, f32[2,256,2,256]{3,1,2,0:T(8,128)}, u32[]{:S(2)}) copy-start(f32[2,256,2,256]{3,1,2,0:T(8,128)} %copy-done.11) | copy-start | bytes 3145732
  222.0 58.8 %all-gather.15.cloned.1.call-start = ((), (), s32[]{:S(2)}) async-start(), calls=%async_computation.3 | async-start | bytes 1310720 | tf_op jit(solution)/shard_map/all_gather | solution.py:102
  224.3 7.6 %copy-start.7 = (f32[1536,256]{0,1:T(8,128)S(1)}, f32[1536,256]{0,1:T(8,128)}, u32[]{:S(2)}) copy-start(f32[1536,256]{0,1:T(8,128)} %copy.259) | copy-start | bytes 4718596
  226.1 5.8 %copy-start = (f32[2048,2048]{1,0:T(8,128)}, f32[2048,2048]{1,0:T(8,128)S(1)}, u32[]{:S(2)}) copy-start(f32[2048,2048]{1,0:T(8,128)S(1)} %fusion.20) | copy-start | bytes 50331652
  247.8 109.8 %all-gather.13.cloned.1.call-start = ((), (), s32[]{:S(2)}) async-start(), calls=%async_computation.2 | async-start | bytes 8650752 | tf_op jit(solution)/shard_map/all_gather | solution.py:21
  260.2 17.2 %copy-start.22 = (f32[128,128]{1,0:T(8,128)}, f32[128,128]{1,0:T(8,128)S(1)}, u32[]{:S(2)}) copy-start(f32[128,128]{1,0:T(8,128)S(1)} %convolution_divide_fusion.11) | copy-start | bytes 196612
  275.9 4.9 copy-start.42
  275.9 4.9 copy-start.44
  277.2 5.1 copy-start.45
  277.4 5.2 copy-start.47
  282.2 2.8 copy-start.21
  283.6 4.3 copy-start.9
  285.5 3.8 copy-start.8
  315.3 27.6 %copy-start.23 = (f32[128,128]{1,0:T(8,128)S(1)}, f32[128,128]{1,0:T(8,128)}, u32[]{:S(2)}) copy-start(f32[128,128]{1,0:T(8,128)} %copy-done.22) | copy-start | bytes 196612
  335.6 7.3 %copy-start.28 = (f32[256,256]{1,0:T(8,128)S(1)}, f32[256,256]{1,0:T(8,128)}, u32[]{:S(2)}) copy-start(f32[256,256]{1,0:T(8,128)} %convolution_subtract_fusion.3) | copy-start | bytes 786436
  335.6 7.3 %copy-start.46 = (f32[128,128]{1,0:T(8,128)S(1)}, f32[128,128]{1,0:T(8,128)}, u32[]{:S(2)}) copy-start(f32[128,128]{1,0:T(8,128)} %copy-done.45) | copy-start | bytes 196612
  335.6 7.3 %copy-start.48 = (f32[128,128]{1,0:T(8,128)S(1)}, f32[128,128]{1,0:T(8,128)}, u32[]{:S(2)}) copy-start(f32[128,128]{1,0:T(8,128)} %copy-done.47) | copy-start | bytes 196612
  341.4 3.8 copy-start.25
  343.4 4.0 copy-start.62
  343.4 4.0 copy-start.69
  371.5 16.4 %copy-start.38 = (f32[256,256]{0,1:T(8,128)S(1)}, f32[256,256]{0,1:T(8,128)}, u32[]{:S(2)}) copy-start(f32[256,256]{0,1:T(8,128)} %copy-done.37) | copy-start | bytes 786436
  405.8 4.4 copy-start.19
  406.0 4.7 copy-start.66
  408.8 2.9 copy-start.14
  428.9 5.0 copy-start.40
  431.3 24.8 %copy-start.15 = (f32[2,256,1,256]{3,1,0,2:T(8,128)S(1)}, f32[2,256,1,256]{3,1,0,2:T(8,128)}, u32[]{:S(2)}) copy-start(f32[2,256,1,256]{3,1,0,2:T(8,128)} %slice.401) | copy-start | bytes 1572868
  456.1 4.8 copy-start.27
  461.5 2.8 copy-start.64
  461.6 3.8 copy-start.16
  469.1 15.7 %copy-start.13 = (f32[512,256]{0,1:T(8,128)}, f32[512,256]{0,1:T(8,128)S(1)}, u32[]{:S(2)}) copy-start(f32[512,256]{0,1:T(8,128)S(1)} %fusion.44) | copy-start | bytes 1572868
  485.5 16.1 %copy-start.29 = (f32[128,128]{1,0:T(8,128)}, f32[128,128]{1,0:T(8,128)S(1)}, u32[]{:S(2)}) copy-start(f32[128,128]{1,0:T(8,128)S(1)} %convolution_divide_fusion.3) | copy-start | bytes 196612
  500.6 9.2 %copy-start.10 = (f32[4,256,1,256]{3,1,2,0:T(8,128)S(1)}, f32[4,256,1,256]{3,1,2,0:T(8,128)}, u32[]{:S(2)}) copy-start(f32[4,256,1,256]{3,1,2,0:T(8,128)} %all-gather.11.cloned.1.call-done) | copy-start | bytes 3145732
  508.3 4.0 copy-start.30
  509.9 3.7 copy-start.17
  519.2 16.6 %copy-start.33 = (f32[256,256]{0,1:T(8,128)S(1)}, f32[256,256]{0,1:T(8,128)}, u32[]{:S(2)}) copy-start(f32[256,256]{0,1:T(8,128)} %copy-done.32) | copy-start | bytes 786436
  553.8 3.5 copy-start.50
  (36 other events, 47.2 us)
Sparse Core Ops, SparseCore 0:
  11.3 80.1 all-gather.8
  222.1 26.5 all-gather.10
  250.2 27.3 all-gather.14
  280.4 77.1 all-gather.12

commit v4 on v2

--- a/solution.py
+++ b/solution.py
@@ -122,7 +122,7 @@
         diag = jnp.tril(diag) + jnp.tril(diag, -1).T
         lkk, linv = factor_diag(diag)
         below = mm(panel[tile:], linv.T)
-        factor = factor.at[k * tile:, cols].set(jnp.concatenate([lkk, below], axis=0))
+        factor = lax.dynamic_update_slice(factor, jnp.concatenate([lkk, below], axis=0), (k * tile, k * tile))
 
     outs = []
     for slot in range(slot_count):

time: 544 us -> 545 us (level)
    scatter x1 -> x0, local copies, waits for them, and re-layouts: 8.98 us -> none  [shards(): factor.at[k * tile:, cols].set(jnp.concatenate([lkk, below], axis=0))]
    dynamic_update_slice x0 -> x1, local copies, waits for them, and re-layouts: none -> 8.98 us  [shards(): lax.dynamic_update_slice(factor, jnp.concatenate([lkk, below], axis=0), (...]
    dynamic_update_slice x0 -> x7, other arithmetic: none -> 8.6 us  [shards(): lax.dynamic_update_slice(factor, jnp.concatenate([lkk, below], axis=0), (...]
    scatter x7 -> x0, other arithmetic: 8.6 us -> none  [shards(): factor.at[k * tile:, cols].set(jnp.concatenate([lkk, below], axis=0))]
    unnamed x63 -> x65, local copies, waits for them, and re-layouts: 20.3 us -> 19.8 us
where the time goes in v4:
time: 545 us; the launch traced here: 534 us
  other arithmetic  233 us (43%)
  waiting for transfers between devices  105 us (19%)
  matrix products  99.8 us (18%)
  local copies, waits for them, and re-layouts  78.5 us (14%)
  between operations  18.3 us (3%)
    another operation x24, other arithmetic, factor_diag(): l11 = jnp.tril(lax.linalg.cholesky(s11, symmetrize_input=True))  101 us
    dot_general x239, matrix products, mm(): jnp.dot(a, b, precision=precision, preferred_element_type=jnp.float32)  99.8 us
    another operation x24, other arithmetic, factor_diag(): lax.linalg.cholesky(diag[:half, :half], symmetrize_input=False)  99.7 us
    all_gather x2, waiting for transfers between devices, separator_panels(): pieces.append(lax.all_gather(piece, ('col', 'row'), axis=0))  80.2 us
    all_gather x2, waiting for transfers between devices, gather_tail(): tail_pieces.append(lax.all_gather(piece, 'col', axis=0))  24.4 us
    unnamed x65, local copies, waits for them, and re-layouts  19.8 us
    slice x8, local copies, waits for them, and re-layouts, panel(): pieces[k // n_col][base + k:base + n_row]  13.2 us
    reduce_sum x16, other arithmetic, lower_inverse(): diag = jnp.sum(lower * eye, axis=1)  11.5 us
  transfers between devices with their start and end apart: 4, of which 2 were waited for; matrix products, arithmetic and copies ran while one was open for 28% of the time, Pallas kernels for 0%

profile of v4, /device:TPU:0, one launch (start us, length us, event | category | flops | bytes accessed | tf_op | source)
XLA Modules:
  0.0 534.1 jit_solution(11268324794410434214)
XLA Ops:
  11.2 80.2 %all-gather.9.cloned.1.call-done = f32[32,256,1,256]{3,1,2,0:T(8,128)} async-done(((f32[1,256,1,256]{3,1,2,0:T(8,128)}), f32[32,256,1,256]{3,1,2,0:T(8,128)}) %all-gather.9.cloned.1.call-update) | async-done | bytes 8388624 | tf_op jit(solution)/shard_map/all_gather | solution.py:21
  91.5 2.8 slice.364
  94.2 2.0 slice.355
  99.4 4.8 copy.516
  108.2 1.8 copy.459
  114.2 1.8 copy.323
  118.0 11.7 %custom-call.18 = f32[128,128]{1,0:T(8,128)S(1)} custom-call(f32[128,128]{1,0:T(8,128)S(1)} %copy.324), custom_call_target="Cholesky" | custom-call | tf_op jit(solution)/shard_map/cholesky/custom-call.1 | solution.py:62
  138.7 12.5 %custom-call.19 = f32[128,128]{1,0:T(8,128)S(1)} custom-call(f32[128,128]{1,0:T(8,128)} %copy.328), custom_call_target="Cholesky" | custom-call | tf_op jit(solution)/shard_map/cholesky/custom-call.1 | solution.py:66
  154.3 1.7 fusion.309
  156.8 2.8 copy.363
  159.6 2.0 copy.349
  161.6 1.7 copy.335
  165.6 24.4 %all-gather.11.cloned.1.call-done = f32[4,256,1,256]{3,1,2,0:T(8,128)} async-done(((f32[1,256,1,256]{3,1,2,0:T(8,128)}), f32[4,256,1,256]{3,1,2,0:T(8,128)}) %all-gather.11.cloned.1.call-update) | async-done | bytes 1048592 | tf_op jit(solution)/shard_map/all_gather | solution.py:104
  190.0 2.0 fusion.299
  192.2 3.5 fusion.24
  199.4 11.7 %custom-call.20 = f32[128,128]{1,0:T(8,128)S(1)} custom-call(f32[128,128]{1,0:T(8,128)S(1)} %copy.339), custom_call_target="Cholesky" | custom-call | tf_op jit(solution)/shard_map/cholesky/custom-call.1 | solution.py:62
  216.1 11.9 %custom-call.21 = f32[128,128]{1,0:T(8,128)S(1)} custom-call(f32[128,128]{1,0:T(8,128)S(1)} %copy.343), custom_call_target="Cholesky" | custom-call | tf_op jit(solution)/shard_map/cholesky/custom-call.1 | solution.py:66
  233.0 5.8 %fusion.29 = f32[1792,256]{1,0:T(8,128)} fusion(f32[2048,256]{0,1:T(8,128)} %copy-done.1, f32[128,128]{1,0:T(8,128)S(1)} %convolution_divide_fusion.13, f32[128,128]{1,0:T(8,128)S(1)} %convolution_divide_fusion.12, f32[128,128]{1,0:T(8,128)S(1)} %convolution_negate_fusion.6), kind=kOutput, calls=%fused_computation.143 | convolution fusion | flops 1409548288 | bytes 3866624 | tf_op jit(solution)/shard_map/dot_general | solution.py:10
  240.3 1.9 copy.518
  243.3 1.7 slice_add_fusion.1
  245.0 9.0 %dynamic_update_slice.24 = f32[2304,2048]{1,0:T(8,128)} pad(f32[2304,256]{1,0:T(8,128)S(1)} %copy-done.2, f32[]{:T(128)} %constant.154.clone.1), padding=0_0x0_1792 | pad | bytes 21233668 | tf_op jit(solution)/shard_map/dynamic_update_slice | solution.py:125
  256.2 3.8 fusion.18
  261.1 11.9 %custom-call.22 = f32[128,128]{1,0:T(8,128)S(1)} custom-call(f32[128,128]{1,0:T(8,128)S(1)} %copy.353), custom_call_target="Cholesky" | custom-call | tf_op jit(solution)/shard_map/cholesky/custom-call.1 | solution.py:62
  276.8 1.8 copy.464
  282.7 11.7 %custom-call.23 = f32[128,128]{1,0:T(8,128)S(1)} custom-call(f32[128,128]{1,0:T(8,128)S(1)} %copy.357), custom_call_target="Cholesky" | custom-call | tf_op jit(solution)/shard_map/cholesky/custom-call.1 | solution.py:66
  299.0 3.1 fusion.34
  304.1 4.7 fusion.15
  309.1 11.7 %custom-call.24 = f32[128,128]{1,0:T(8,128)S(1)} custom-call(f32[128,128]{1,0:T(8,128)S(1)} %copy.367), custom_call_target="Cholesky" | custom-call | tf_op jit(solution)/shard_map/cholesky/custom-call.1 | solution.py:62
  325.8 11.9 %custom-call.25 = f32[128,128]{1,0:T(8,128)S(1)} custom-call(f32[128,128]{1,0:T(8,128)S(1)} %copy.371), custom_call_target="Cholesky" | custom-call | tf_op jit(solution)/shard_map/cholesky/custom-call.1 | solution.py:66
  342.3 2.3 fusion.42
  345.9 1.9 slice.394
  350.6 5.0 fusion.12
  356.1 11.7 %custom-call.26 = f32[128,128]{1,0:T(8,128)S(1)} custom-call(f32[128,128]{1,0:T(8,128)S(1)} %copy.381), custom_call_target="Cholesky" | custom-call | tf_op jit(solution)/shard_map/cholesky/custom-call.1 | solution.py:62
  372.7 11.7 %custom-call.27 = f32[128,128]{1,0:T(8,128)S(1)} custom-call(f32[128,128]{1,0:T(8,128)S(1)} %copy.385), custom_call_target="Cholesky" | custom-call | tf_op jit(solution)/shard_map/cholesky/custom-call.1 | solution.py:66
  389.0 1.8 fusion.56
  392.1 5.1 fusion.36
  397.6 12.1 %custom-call.28 = f32[128,128]{1,0:T(8,128)S(1)} custom-call(f32[128,128]{1,0:T(8,128)S(1)} %copy.392), custom_call_target="Cholesky" | custom-call | tf_op jit(solution)/shard_map/cholesky/custom-call.1 | solution.py:62
  414.4 11.7 %custom-call.29 = f32[128,128]{1,0:T(8,128)S(1)} custom-call(f32[128,128]{1,0:T(8,128)S(1)} %copy.396), custom_call_target="Cholesky" | custom-call | tf_op jit(solution)/shard_map/cholesky/custom-call.1 | solution.py:66
  432.9 5.1 fusion.44
  438.3 11.7 %custom-call.30 = f32[128,128]{1,0:T(8,128)S(1)} custom-call(f32[128,128]{1,0:T(8,128)S(1)} %copy.406), custom_call_target="Cholesky" | custom-call | tf_op jit(solution)/shard_map/cholesky/custom-call.1 | solution.py:62
  454.8 11.7 %custom-call.31 = f32[128,128]{1,0:T(8,128)S(1)} custom-call(f32[128,128]{1,0:T(8,128)S(1)} %fusion.218), custom_call_target="Cholesky" | custom-call | tf_op jit(solution)/shard_map/cholesky/custom-call.1 | solution.py:66
  474.6 4.2 fusion.49
  479.2 11.7 %custom-call.32 = f32[128,128]{1,0:T(8,128)S(1)} custom-call(f32[128,128]{1,0:T(8,128)S(1)} %copy.417), custom_call_target="Cholesky" | custom-call | tf_op jit(solution)/shard_map/cholesky/custom-call.1 | solution.py:62
  495.8 11.9 %custom-call.33 = f32[128,128]{1,0:T(8,128)S(1)} custom-call(f32[128,128]{1,0:T(8,128)S(1)} %broadcast_multiply_fusion.1), custom_call_target="Cholesky" | custom-call | tf_op jit(solution)/shard_map/cholesky/custom-call.1 | solution.py:66
  514.0 3.9 constant_dynamic-slice_fusion.3
  517.9 2.9 copy.424
  522.1 1.9 copy.426
  525.4 1.8 copy.428
  (454 shorter events, 127.3 us)
Async XLA Ops:
  6.5 84.9 %all-gather.9.cloned.1.call-start = ((), (), s32[]{:S(2)}) async-start(), calls=%async_computation | async-start | bytes 8650752 | tf_op jit(solution)/shard_map/all_gather | solution.py:21
  9.5 1.0 copy-start.7
  11.2 178.8 %all-gather.11.cloned.1.call-start = ((), (), s32[]{:S(2)}) async-start(), calls=%async_computation.1 | async-start | bytes 1310720 | tf_op jit(solution)/shard_map/all_gather | solution.py:104
  91.5 6.4 %copy-start = (f32[32,256,1,256]{3,1,2,0:T(8,128)S(1)}, f32[32,256,1,256]{3,1,2,0:T(8,128)}, u32[]{:S(2)}) copy-start(f32[32,256,1,256]{3,1,2,0:T(8,128)} %all-gather.9.cloned.1.call-done) | copy-start | bytes 25165828
  99.4 6.0 %copy-start.8 = (f32[2,256,2,256]{3,1,2,0:T(8,128)S(1)}, f32[2,256,2,256]{3,1,2,0:T(8,128)}, u32[]{:S(2)}) copy-start(f32[2,256,2,256]{3,1,2,0:T(8,128)} %copy-done.7) | copy-start | bytes 3145732
  117.1 0.7 copy-start.16
  129.7 4.8 copy-start.17
  131.0 0.6 copy-start.20
  133.9 0.6 copy-start.18
  152.8 0.6 copy-start.22
  161.6 2.0 copy-start.26
  161.6 3.8 copy-start.25
  163.3 77.0 %all-gather.13.cloned.1.call-start = ((), (), s32[]{:S(2)}) async-start(), calls=%async_computation.2 | async-start | bytes 1310720 | tf_op jit(solution)/shard_map/all_gather | solution.py:104
  164.0 28.1 %copy-start.19 = (f32[128,128]{1,0:T(8,128)S(1)}, f32[128,128]{1,0:T(8,128)}, u32[]{:S(2)}) copy-start(f32[128,128]{1,0:T(8,128)} %copy-done.18) | copy-start | bytes 196612
  165.1 180.8 %all-gather.15.cloned.1.call-start = ((), (), s32[]{:S(2)}) async-start(), calls=%async_computation.3 | async-start | bytes 8650752 | tf_op jit(solution)/shard_map/all_gather | solution.py:21
  192.2 3.5 copy-start.3
  196.7 1.4 copy-start.1
  232.5 6.2 %copy-start.21 = (f32[128,128]{1,0:T(8,128)S(1)}, f32[128,128]{1,0:T(8,128)}, u32[]{:S(2)}) copy-start(f32[128,128]{1,0:T(8,128)} %copy-done.20) | copy-start | bytes 196612
  232.5 6.2 %copy-start.23 = (f32[128,128]{1,0:T(8,128)S(1)}, f32[128,128]{1,0:T(8,128)}, u32[]{:S(2)}) copy-start(f32[128,128]{1,0:T(8,128)} %copy-done.22) | copy-start | bytes 196612
  232.5 6.2 %copy-start.24 = (f32[128,128]{1,0:T(8,128)S(1)}, f32[128,128]{1,0:T(8,128)}, u32[]{:S(2)}) copy-start(f32[128,128]{1,0:T(8,128)} %copy.329) | copy-start | bytes 196612
  240.3 4.7 copy-start.2
  245.0 9.0 %copy-start.4 = (f32[1792,256]{1,0:T(8,128)S(1)}, f32[1792,256]{1,0:T(8,128)}, u32[]{:S(2)}) copy-start(f32[1792,256]{1,0:T(8,128)} %fusion.29) | copy-start | bytes 5505028
  254.0 2.2 copy-start.5
  260.0 14.3 %copy-start.9 = (f32[4,256,1,256]{3,1,2,0:T(8,128)S(1)}, f32[4,256,1,256]{3,1,2,0:T(8,128)}, u32[]{:S(2)}) copy-start(f32[4,256,1,256]{3,1,2,0:T(8,128)} %all-gather.13.cloned.1.call-done) | copy-start | bytes 3145732
  260.2 15.4 %copy-start.13 = (f32[1,256,1,256]{3,1,2,0:T(8,128)S(1)}, f32[1,256,1,256]{3,1,2,0:T(8,128)}, u32[]{:S(2)}) copy-start(f32[1,256,1,256]{3,1,2,0:T(8,128)} %get-tuple-element.44) | copy-start | bytes 786436
  260.3 0.7 copy-start.14
  275.7 6.2 %copy-start.15 = (f32[256,256]{0,1:T(8,128)S(1)}, f32[256,256]{0,1:T(8,128)}, u32[]{:S(2)}) copy-start(f32[256,256]{0,1:T(8,128)} %copy-done.14) | copy-start | bytes 786436
  302.2 1.9 copy-start.6
  389.0 3.0 copy-start.12
  411.7 16.8 %copy-start.10 = (f32[2,256,1,256]{3,1,0,2:T(8,128)S(1)}, f32[2,256,1,256]{3,1,0,2:T(8,128)}, u32[]{:S(2)}) copy-start(f32[2,256,1,256]{3,1,0,2:T(8,128)} %slice.394) | copy-start | bytes 1572868
  430.5 2.4 copy-start.11
Sparse Core Ops, SparseCore 0:
  11.3 80.1 all-gather.8
  163.5 26.5 all-gather.10
  191.6 27.4 all-gather.12
  245.1 77.3 all-gather.14

commit v5 on v2

--- a/solution.py
+++ b/solution.py
@@ -48,12 +48,13 @@
     diag = jnp.sum(lower * eye, axis=1)
     strict = jnp.tril(jnp.ones((size, size), jnp.bool_), -1)
     power = jnp.where(strict, -lower / diag[:, None], 0.0)
-    product = eye + power
-    span = 2
-    while span < size:
-        power = mm(power, power)
-        product = mm(product, eye + power)
-        span *= 2
+    product = eye
+    covered = 1
+    while covered < size:
+        both = mm(jnp.concatenate([product, power], axis=0), eye + power)
+        product = both[:size]
+        power = both[size:] - power
+        covered *= 2
     return product / diag[None, :]
 
 

time: 544 us -> 525 us (0.965)
  matrix products: 98.3 us -> 83.9 us
  waiting for transfers between devices: 104 us -> 90 us
  other arithmetic: 233 us -> 245 us
    dot_general x239 -> x159, matrix products: 98.3 us -> 83.9 us  [mm(): jnp.dot(a, b, precision=precision, preferred_element_type=jnp.float32)]
    all_gather x2, waiting for transfers between devices: 24.4 us -> 10.3 us  [gather_tail(): tail_pieces.append(lax.all_gather(piece, 'col', axis=0))]
    another operation x24, other arithmetic: 100 us -> 108 us  [factor_diag(): l11 = jnp.tril(lax.linalg.cholesky(s11, symmetrize_input=True))]
    unnamed x63 -> x57, local copies, waits for them, and re-layouts: 20.3 us -> 21.1 us
  transfers between devices with their start and end apart: 4 -> 4, of which waited for: 2 -> 2; matrix products, arithmetic and copies ran while one was open for 28% -> 32% of each run, Pallas kernels for 0% -> 0%
where the time goes in v5:
time: 525 us; the launch traced here: 517 us
  other arithmetic  245 us (47%)
  waiting for transfers between devices  90 us (17%)
  matrix products  83.9 us (16%)
  local copies, waits for them, and re-layouts  79.1 us (15%)
  between operations  18.7 us (4%)
    another operation x24, other arithmetic, factor_diag(): l11 = jnp.tril(lax.linalg.cholesky(s11, symmetrize_input=True))  108 us
    another operation x24, other arithmetic, factor_diag(): lax.linalg.cholesky(diag[:half, :half], symmetrize_input=False)  101 us
    dot_general x159, matrix products, mm(): jnp.dot(a, b, precision=precision, preferred_element_type=jnp.float32)  83.9 us
    all_gather x2, waiting for transfers between devices, separator_panels(): pieces.append(lax.all_gather(piece, ('col', 'row'), axis=0))  79.6 us
    unnamed x57, local copies, waits for them, and re-layouts  21.1 us
    slice x8, local copies, waits for them, and re-layouts, panel(): pieces[k // n_col][base + k:base + n_row]  13 us
    reduce_sum x16, other arithmetic, lower_inverse(): diag = jnp.sum(lower * eye, axis=1)  11.9 us
  transfers between devices with their start and end apart: 4, of which 2 were waited for; matrix products, arithmetic and copies ran while one was open for 32% of the time, Pallas kernels for 0%

profile of v5, /device:TPU:0, one launch (start us, length us, event | category | flops | bytes accessed | tf_op | source)
XLA Modules:
  0.0 516.9 jit_solution(12734035649716741824)
XLA Ops:
  11.9 79.6 %all-gather.9.cloned.1.call-done = f32[32,256,1,256]{3,1,2,0:T(8,128)} async-done(((f32[1,256,1,256]{3,1,2,0:T(8,128)}), f32[32,256,1,256]{3,1,2,0:T(8,128)}) %all-gather.9.cloned.1.call-update) | async-done | bytes 8388624 | tf_op jit(solution)/shard_map/all_gather | solution.py:21
  93.1 3.0 slice.1417
  96.1 3.0 slice.1384
  99.2 4.9 copy.516
  108.2 1.8 copy.459
  112.5 1.7 add_bitcast_fusion
  114.2 1.8 copy.323
  118.5 12.5 %custom-call.18 = f32[128,128]{1,0:T(8,128)S(1)} custom-call(f32[128,128]{1,0:T(8,128)} %copy.324), custom_call_target="Cholesky" | custom-call | tf_op jit(solution)/shard_map/cholesky/custom-call.1 | solution.py:63
  138.7 3.1 copy.349
  141.8 2.8 copy.335
  145.1 11.7 %custom-call.19 = f32[128,128]{1,0:T(8,128)S(1)} custom-call(f32[128,128]{1,0:T(8,128)S(1)} %copy.328), custom_call_target="Cholesky" | custom-call | tf_op jit(solution)/shard_map/cholesky/custom-call.1 | solution.py:67
  161.0 10.3 %all-gather.11.cloned.1.call-done = f32[4,256,1,256]{3,1,2,0:T(8,128)} async-done(((f32[1,256,1,256]{3,1,2,0:T(8,128)}), f32[4,256,1,256]{3,1,2,0:T(8,128)}) %all-gather.11.cloned.1.call-update) | async-done | bytes 1048592 | tf_op jit(solution)/shard_map/all_gather | solution.py:105
  171.3 2.0 fusion.686
  173.5 1.9 fusion.26
  180.7 11.7 %custom-call.20 = f32[128,128]{1,0:T(8,128)S(1)} custom-call(f32[128,128]{1,0:T(8,128)S(1)} %copy.339), custom_call_target="Cholesky" | custom-call | tf_op jit(solution)/shard_map/cholesky/custom-call.1 | solution.py:63
  196.9 20.5 %custom-call.21 = f32[128,128]{1,0:T(8,128)S(1)} custom-call(f32[128,128]{1,0:T(8,128)S(1)} %copy.343), custom_call_target="Cholesky" | custom-call | tf_op jit(solution)/shard_map/cholesky/custom-call.1 | solution.py:67
  221.8 5.8 %fusion.31 = f32[1792,256]{1,0:T(8,128)} fusion(f32[2048,256]{0,1:T(8,128)} %copy-done.1, f32[128,128]{1,0:T(8,128)S(1)} %convolution_divide_fusion.13, f32[128,128]{1,0:T(8,128)S(1)} %convolution_divide_fusion.12, f32[128,128]{1,0:T(8,128)S(1)} %convolution_negate_fusion.6), kind=kOutput, calls=%fused_computation.145 | convolution fusion | flops 1409548288 | bytes 3866624 | tf_op jit(solution)/shard_map/dot_general | solution.py:10
  227.5 1.8 copy.518
  230.6 1.7 slice_add_fusion.1
  232.3 9.0 %scatter.26 = f32[2304,2048]{1,0:T(8,128)} pad(f32[2304,256]{1,0:T(8,128)S(1)} %fusion.22, f32[]{:T(128)} %constant.352.clone.1), padding=0_0x0_1792 | pad | bytes 21233668 | tf_op jit(solution)/shard_map/scatter | solution.py:126
  243.5 3.8 fusion.18
  248.4 11.9 %custom-call.22 = f32[128,128]{1,0:T(8,128)S(1)} custom-call(f32[128,128]{1,0:T(8,128)S(1)} %copy.353), custom_call_target="Cholesky" | custom-call | tf_op jit(solution)/shard_map/cholesky/custom-call.1 | solution.py:63
  265.4 1.8 copy.464
  267.1 1.8 copy.463
  270.6 11.7 %custom-call.23 = f32[128,128]{1,0:T(8,128)S(1)} custom-call(f32[128,128]{1,0:T(8,128)S(1)} %copy.357), custom_call_target="Cholesky" | custom-call | tf_op jit(solution)/shard_map/cholesky/custom-call.1 | solution.py:67
  286.4 3.1 fusion.36
  291.5 4.7 fusion.15
  296.5 11.7 %custom-call.24 = f32[128,128]{1,0:T(8,128)S(1)} custom-call(f32[128,128]{1,0:T(8,128)S(1)} %copy.367), custom_call_target="Cholesky" | custom-call | tf_op jit(solution)/shard_map/cholesky/custom-call.1 | solution.py:63
  312.7 11.9 %custom-call.25 = f32[128,128]{1,0:T(8,128)S(1)} custom-call(f32[128,128]{1,0:T(8,128)S(1)} %copy.371), custom_call_target="Cholesky" | custom-call | tf_op jit(solution)/shard_map/cholesky/custom-call.1 | solution.py:67
  328.7 2.3 fusion.44
  332.3 1.9 slice.1552
  337.0 5.1 fusion.12
  342.4 11.7 %custom-call.26 = f32[128,128]{1,0:T(8,128)S(1)} custom-call(f32[128,128]{1,0:T(8,128)S(1)} %copy.381), custom_call_target="Cholesky" | custom-call | tf_op jit(solution)/shard_map/cholesky/custom-call.1 | solution.py:63
  359.1 11.7 %custom-call.27 = f32[128,128]{1,0:T(8,128)S(1)} custom-call(f32[128,128]{1,0:T(8,128)S(1)} %copy.385), custom_call_target="Cholesky" | custom-call | tf_op jit(solution)/shard_map/cholesky/custom-call.1 | solution.py:67
  374.6 1.8 fusion.58
  377.7 5.1 fusion.38
  383.2 12.1 %custom-call.28 = f32[128,128]{1,0:T(8,128)S(1)} custom-call(f32[128,128]{1,0:T(8,128)S(1)} %copy.392), custom_call_target="Cholesky" | custom-call | tf_op jit(solution)/shard_map/cholesky/custom-call.1 | solution.py:63
  400.2 11.7 %custom-call.29 = f32[128,128]{1,0:T(8,128)S(1)} custom-call(f32[128,128]{1,0:T(8,128)S(1)} %copy.396), custom_call_target="Cholesky" | custom-call | tf_op jit(solution)/shard_map/cholesky/custom-call.1 | solution.py:67
  417.7 5.1 fusion.46
  423.1 11.7 %custom-call.30 = f32[128,128]{1,0:T(8,128)S(1)} custom-call(f32[128,128]{1,0:T(8,128)S(1)} %copy.406), custom_call_target="Cholesky" | custom-call | tf_op jit(solution)/shard_map/cholesky/custom-call.1 | solution.py:63
  440.6 11.7 %custom-call.31 = f32[128,128]{1,0:T(8,128)S(1)} custom-call(f32[128,128]{1,0:T(8,128)S(1)} %fusion.508), custom_call_target="Cholesky" | custom-call | tf_op jit(solution)/shard_map/cholesky/custom-call.1 | solution.py:67
  458.4 4.2 fusion.51
  463.0 11.7 %custom-call.32 = f32[128,128]{1,0:T(8,128)S(1)} custom-call(f32[128,128]{1,0:T(8,128)S(1)} %copy.417), custom_call_target="Cholesky" | custom-call | tf_op jit(solution)/shard_map/cholesky/custom-call.1 | solution.py:63
  479.4 11.9 %custom-call.33 = f32[128,128]{1,0:T(8,128)S(1)} custom-call(f32[128,128]{1,0:T(8,128)S(1)} %broadcast_multiply_fusion.1), custom_call_target="Cholesky" | custom-call | tf_op jit(solution)/shard_map/cholesky/custom-call.1 | solution.py:67
  496.7 3.9 constant_dynamic-slice_fusion.3
  500.6 2.9 copy.424
  504.9 1.9 copy.426
  508.1 1.8 copy.428
  (480 shorter events, 115.1 us)
Async XLA Ops:
  6.5 85.0 %all-gather.9.cloned.1.call-start = ((), (), s32[]{:S(2)}) async-start(), calls=%async_computation | async-start | bytes 8650752 | tf_op jit(solution)/shard_map/all_gather | solution.py:21
  9.5 1.0 copy-start.6
  11.2 160.1 %all-gather.11.cloned.1.call-start = ((), (), s32[]{:S(2)}) async-start(), calls=%async_computation.1 | async-start | bytes 1310720 | tf_op jit(solution)/shard_map/all_gather | solution.py:105
  91.5 7.5 %copy-start = (f32[32,256,1,256]{3,1,2,0:T(8,128)S(1)}, f32[32,256,1,256]{3,1,2,0:T(8,128)}, u32[]{:S(2)}) copy-start(f32[32,256,1,256]{3,1,2,0:T(8,128)} %all-gather.9.cloned.1.call-done) | copy-start | bytes 25165828
  99.2 6.2 %copy-start.7 = (f32[2,256,2,256]{3,1,2,0:T(8,128)S(1)}, f32[2,256,2,256]{3,1,2,0:T(8,128)}, u32[]{:S(2)}) copy-start(f32[2,256,2,256]{3,1,2,0:T(8,128)} %copy-done.6) | copy-start | bytes 3145732
  117.1 0.7 copy-start.17
  131.1 4.3 copy-start.18
  132.5 2.0 copy-start.10
  134.7 0.6 copy-start.19
  141.8 3.1 copy-start.21
  144.6 14.8 %copy-start.20 = (f32[128,128]{1,0:T(8,128)S(1)}, f32[128,128]{1,0:T(8,128)}, u32[]{:S(2)}) copy-start(f32[128,128]{1,0:T(8,128)} %copy-done.19) | copy-start | bytes 196612
  144.6 82.9 %all-gather.13.cloned.1.call-start = ((), (), s32[]{:S(2)}) async-start(), calls=%async_computation.2 | async-start | bytes 1310720 | tf_op jit(solution)/shard_map/all_gather | solution.py:105
  160.6 171.7 %all-gather.15.cloned.1.call-start = ((), (), s32[]{:S(2)}) async-start(), calls=%async_computation.3 | async-start | bytes 8650752 | tf_op jit(solution)/shard_map/all_gather | solution.py:21
  173.5 2.0 copy-start.11
  173.5 2.0 copy-start.22
  175.5 1.5 copy-start.2
  178.0 1.4 copy-start.1
  232.3 9.0 %copy-start.3 = (f32[1792,256]{1,0:T(8,128)S(1)}, f32[1792,256]{1,0:T(8,128)}, u32[]{:S(2)}) copy-start(f32[1792,256]{1,0:T(8,128)} %fusion.31) | copy-start | bytes 5505028
  241.3 2.2 copy-start.4
  247.3 15.8 %copy-start.8 = (f32[4,256,1,256]{3,1,2,0:T(8,128)S(1)}, f32[4,256,1,256]{3,1,2,0:T(8,128)}, u32[]{:S(2)}) copy-start(f32[4,256,1,256]{3,1,2,0:T(8,128)} %all-gather.13.cloned.1.call-done) | copy-start | bytes 3145732
  247.6 0.7 copy-start.15
  262.1 2.0 copy-start.14
  264.1 5.6 %copy-start.16 = (f32[256,256]{0,1:T(8,128)S(1)}, f32[256,256]{0,1:T(8,128)}, u32[]{:S(2)}) copy-start(f32[256,256]{0,1:T(8,128)} %copy-done.15) | copy-start | bytes 786436
  289.5 1.9 copy-start.5
  374.6 3.1 copy-start.13
  397.2 2.6 copy-start.9
  415.4 2.3 copy-start.12
Sparse Core Ops, SparseCore 0:
  11.3 80.1 all-gather.8
  144.7 26.5 all-gather.10
  172.9 27.4 all-gather.12
  232.4 77.2 all-gather.14

commit v6 on v5

--- a/solution.py
+++ b/solution.py
@@ -122,7 +122,7 @@
             diag = diag + after(tail_sources[0])
         diag = jnp.tril(diag) + jnp.tril(diag, -1).T
         lkk, linv = factor_diag(diag)
-        below = mm(panel[tile:], linv.T)
+        below = mm(panel[tile:], linv.T, lax.Precision.HIGH)
         factor = factor.at[k * tile:, cols].set(jnp.concatenate([lkk, below], axis=0))
 
     outs = []

time: 525 us -> 510 us (0.971)
  starting transfers between devices: 0.39 us -> 12.4 us
  waiting for transfers between devices: 90 us -> 79.7 us
  other arithmetic: 245 us -> 237 us
  matrix products: 83.9 us -> 76.7 us
    all_gather x2, starting transfers between devices: 0.34 us -> 12.4 us  [gather_tail(): tail_pieces.append(lax.all_gather(piece, 'col', axis=0))]
    all_gather x2, waiting for transfers between devices: 10.3 us -> 0.02 us  [gather_tail(): tail_pieces.append(lax.all_gather(piece, 'col', axis=0))]
    another operation x24, other arithmetic: 108 us -> 100 us  [factor_diag(): l11 = jnp.tril(lax.linalg.cholesky(s11, symmetrize_input=True))]
    dot_general x159, matrix products: 83.9 us -> 76.7 us  [mm(): jnp.dot(a, b, precision=precision, preferred_element_type=jnp.float32)]
  transfers between devices with their start and end apart: 4 -> 4, of which waited for: 2 -> 1; matrix products, arithmetic and copies ran while one was open for 32% -> 31% of each run, Pallas kernels for 0% -> 0%
where the time goes in v6:
time: 510 us; the launch traced here: 503 us
  other arithmetic  237 us (46%)
  waiting for transfers between devices  79.7 us (16%)
  local copies, waits for them, and re-layouts  79.5 us (16%)
  matrix products  76.7 us (15%)
  between operations  18.5 us (4%)
  starting transfers between devices  12.4 us (2%)
    another operation x24, other arithmetic, factor_diag(): lax.linalg.cholesky(diag[:half, :half], symmetrize_input=False)  100 us
    another operation x24, other arithmetic, factor_diag(): l11 = jnp.tril(lax.linalg.cholesky(s11, symmetrize_input=True))  100 us
    all_gather x2, waiting for transfers between devices, separator_panels(): pieces.append(lax.all_gather(piece, ('col', 'row'), axis=0))  79.6 us
    dot_general x159, matrix products, mm(): jnp.dot(a, b, precision=precision, preferred_element_type=jnp.float32)  76.7 us
    unnamed x57, local copies, waits for them, and re-layouts  21.1 us
    slice x8, local copies, waits for them, and re-layouts, panel(): pieces[k // n_col][base + k:base + n_row]  13.4 us
    all_gather x2, starting transfers between devices, gather_tail(): tail_pieces.append(lax.all_gather(piece, 'col', axis=0))  12.4 us
    reduce_sum x16, other arithmetic, lower_inverse(): diag = jnp.sum(lower * eye, axis=1)  12.4 us
  transfers between devices with their start and end apart: 4, of which 1 were waited for; matrix products, arithmetic and copies ran while one was open for 31% of the time, Pallas kernels for 0%

profile of v6, /device:TPU:0, one launch (start us, length us, event | category | flops | bytes accessed | tf_op | source)
XLA Modules:
  0.0 503.5 jit_solution(1909838269467687484)
XLA Ops:
  11.9 79.6 %all-gather.9.cloned.1.call-done = f32[32,256,1,256]{3,1,2,0:T(8,128)} async-done(((f32[1,256,1,256]{3,1,2,0:T(8,128)}), f32[32,256,1,256]{3,1,2,0:T(8,128)}) %all-gather.9.cloned.1.call-update) | async-done | bytes 8388624 | tf_op jit(solution)/shard_map/all_gather | solution.py:21
  91.5 1.6 slice.1450
  93.1 3.0 slice.1417
  96.1 3.0 slice.1384
  99.2 4.9 copy.516
  108.2 1.8 copy.459
  112.5 1.7 add_bitcast_fusion
  114.2 1.8 copy.323
  118.5 12.5 %custom-call.18 = f32[128,128]{1,0:T(8,128)S(1)} custom-call(f32[128,128]{1,0:T(8,128)} %copy.324), custom_call_target="Cholesky" | custom-call | tf_op jit(solution)/shard_map/cholesky/custom-call.1 | solution.py:63
  137.2 1.5 copy.363
  138.7 3.1 copy.349
  141.8 2.8 copy.335
  144.6 12.3 %all-gather.13.cloned.1.call-start = ((), (), s32[]{:S(2)}) async-start(), calls=%async_computation.2 | async-start | bytes 1310720 | tf_op jit(solution)/shard_map/all_gather | solution.py:105
  157.2 11.7 %custom-call.19 = f32[128,128]{1,0:T(8,128)S(1)} custom-call(f32[128,128]{1,0:T(8,128)S(1)} %copy.328), custom_call_target="Cholesky" | custom-call | tf_op jit(solution)/shard_map/cholesky/custom-call.1 | solution.py:67
  173.1 2.0 fusion.686
  181.6 11.7 %custom-call.20 = f32[128,128]{1,0:T(8,128)S(1)} custom-call(f32[128,128]{1,0:T(8,128)S(1)} %copy.339), custom_call_target="Cholesky" | custom-call | tf_op jit(solution)/shard_map/cholesky/custom-call.1 | solution.py:63
  197.7 12.1 %custom-call.21 = f32[128,128]{1,0:T(8,128)S(1)} custom-call(f32[128,128]{1,0:T(8,128)S(1)} %copy.343), custom_call_target="Cholesky" | custom-call | tf_op jit(solution)/shard_map/cholesky/custom-call.1 | solution.py:67
  214.3 4.3 fusion.31
  218.6 1.8 copy.518
  221.7 1.7 slice_add_fusion.1
  223.4 9.0 %scatter.26 = f32[2304,2048]{1,0:T(8,128)} pad(f32[2304,256]{1,0:T(8,128)S(1)} %fusion.22, f32[]{:T(128)} %constant.352.clone.1), padding=0_0x0_1792 | pad | bytes 21233668 | tf_op jit(solution)/shard_map/scatter | solution.py:126
  232.4 1.5 fusion.24
  234.5 3.8 fusion.18
  239.5 11.7 %custom-call.22 = f32[128,128]{1,0:T(8,128)S(1)} custom-call(f32[128,128]{1,0:T(8,128)S(1)} %copy.353), custom_call_target="Cholesky" | custom-call | tf_op jit(solution)/shard_map/cholesky/custom-call.1 | solution.py:63
  256.4 1.8 copy.464
  258.2 1.8 copy.463
  261.6 11.7 %custom-call.23 = f32[128,128]{1,0:T(8,128)S(1)} custom-call(f32[128,128]{1,0:T(8,128)S(1)} %copy.357), custom_call_target="Cholesky" | custom-call | tf_op jit(solution)/shard_map/cholesky/custom-call.1 | solution.py:67
  280.8 4.7 fusion.15
  285.9 11.9 %custom-call.24 = f32[128,128]{1,0:T(8,128)S(1)} custom-call(f32[128,128]{1,0:T(8,128)S(1)} %copy.367), custom_call_target="Cholesky" | custom-call | tf_op jit(solution)/shard_map/cholesky/custom-call.1 | solution.py:63
  302.3 11.7 %custom-call.25 = f32[128,128]{1,0:T(8,128)S(1)} custom-call(f32[128,128]{1,0:T(8,128)S(1)} %copy.371), custom_call_target="Cholesky" | custom-call | tf_op jit(solution)/shard_map/cholesky/custom-call.1 | solution.py:67
  320.7 1.9 slice.1552
  322.5 1.6 slice.1519
  325.8 5.0 %fusion.12 = f32[1280,256]{0,1:T(8,128)S(1)} fusion(f32[2304,2048]{1,0:T(8,128)} %fusion.35, f32[256,256]{0,1:T(8,128)} %bitcast.171, f32[1024,256]{0,1:T(8,128)S(1)} %copy.377), kind=kOutput, calls=%fused_computation.12 | convolution fusion | flops 2013921280 | bytes 8912896 | tf_op jit(solution)/shard_map/dot_general | solution.py:10
  331.2 11.7 %custom-call.26 = f32[128,128]{1,0:T(8,128)S(1)} custom-call(f32[128,128]{1,0:T(8,128)S(1)} %copy.381), custom_call_target="Cholesky" | custom-call | tf_op jit(solution)/shard_map/cholesky/custom-call.1 | solution.py:63
  347.7 11.9 %custom-call.27 = f32[128,128]{1,0:T(8,128)S(1)} custom-call(f32[128,128]{1,0:T(8,128)S(1)} %copy.385), custom_call_target="Cholesky" | custom-call | tf_op jit(solution)/shard_map/cholesky/custom-call.1 | solution.py:67
  365.6 5.1 %fusion.38 = f32[1024,256]{1,0:T(8,128)S(1)} fusion(f32[2304,2048]{1,0:T(8,128)} %fusion.43, f32[256,256]{1,0:T(8,128)S(1)} %copy-done.13, f32[768,256]{1,0:T(8,128)S(1)} %bitcast.164), kind=kOutput, calls=%fused_computation.154 | convolution fusion | flops 2013790208 | bytes 8650752 | tf_op jit(solution)/shard_map/dot_general | solution.py:10
  371.1 11.7 %custom-call.28 = f32[128,128]{1,0:T(8,128)S(1)} custom-call(f32[128,128]{1,0:T(8,128)S(1)} %copy.392), custom_call_target="Cholesky" | custom-call | tf_op jit(solution)/shard_map/cholesky/custom-call.1 | solution.py:63
  387.8 11.9 %custom-call.29 = f32[128,128]{1,0:T(8,128)S(1)} custom-call(f32[128,128]{1,0:T(8,128)S(1)} %copy.396), custom_call_target="Cholesky" | custom-call | tf_op jit(solution)/shard_map/cholesky/custom-call.1 | solution.py:67
  405.1 4.9 fusion.46
  410.4 11.7 %custom-call.30 = f32[128,128]{1,0:T(8,128)S(1)} custom-call(f32[128,128]{1,0:T(8,128)S(1)} %copy.406), custom_call_target="Cholesky" | custom-call | tf_op jit(solution)/shard_map/cholesky/custom-call.1 | solution.py:63
  428.3 11.7 %custom-call.31 = f32[128,128]{1,0:T(8,128)S(1)} custom-call(f32[128,128]{1,0:T(8,128)S(1)} %fusion.508), custom_call_target="Cholesky" | custom-call | tf_op jit(solution)/shard_map/cholesky/custom-call.1 | solution.py:67
  445.5 4.2 fusion.51
  450.1 11.9 %custom-call.32 = f32[128,128]{1,0:T(8,128)S(1)} custom-call(f32[128,128]{1,0:T(8,128)S(1)} %copy.417), custom_call_target="Cholesky" | custom-call | tf_op jit(solution)/shard_map/cholesky/custom-call.1 | solution.py:63
  466.7 11.7 %custom-call.33 = f32[128,128]{1,0:T(8,128)S(1)} custom-call(f32[128,128]{1,0:T(8,128)S(1)} %broadcast_multiply_fusion.1), custom_call_target="Cholesky" | custom-call | tf_op jit(solution)/shard_map/cholesky/custom-call.1 | solution.py:67
  483.6 3.9 constant_dynamic-slice_fusion.3
  487.5 2.9 copy.424
  491.7 1.9 copy.426
  495.0 1.8 copy.428
  (480 shorter events, 113.1 us)
Async XLA Ops:
  6.5 85.0 %all-gather.9.cloned.1.call-start = ((), (), s32[]{:S(2)}) async-start(), calls=%async_computation | async-start | bytes 8650752 | tf_op jit(solution)/shard_map/all_gather | solution.py:21
  9.5 1.0 copy-start.6
  11.2 161.9 %all-gather.11.cloned.1.call-start = ((), (), s32[]{:S(2)}) async-start(), calls=%async_computation.1 | async-start | bytes 1310720 | tf_op jit(solution)/shard_map/all_gather | solution.py:105
  91.5 7.5 %copy-start = (f32[32,256,1,256]{3,1,2,0:T(8,128)S(1)}, f32[32,256,1,256]{3,1,2,0:T(8,128)}, u32[]{:S(2)}) copy-start(f32[32,256,1,256]{3,1,2,0:T(8,128)} %all-gather.9.cloned.1.call-done) | copy-start | bytes 25165828
  99.2 6.2 %copy-start.7 = (f32[2,256,2,256]{3,1,2,0:T(8,128)S(1)}, f32[2,256,2,256]{3,1,2,0:T(8,128)}, u32[]{:S(2)}) copy-start(f32[2,256,2,256]{3,1,2,0:T(8,128)} %copy-done.6) | copy-start | bytes 3145732
  117.1 0.7 copy-start.17
  131.1 4.3 copy-start.18
  132.5 2.0 copy-start.10
  134.7 0.6 copy-start.19
  141.8 15.2 %copy-start.21 = (f32[128,128]{0,1:T(8,128)S(1)}, f32[128,128]{0,1:T(8,128)}, u32[]{:S(2)}) copy-start(f32[128,128]{0,1:T(8,128)} %convolution_subtract_fusion.8) | copy-start | bytes 196612
  144.6 26.8 %copy-start.20 = (f32[128,128]{1,0:T(8,128)S(1)}, f32[128,128]{1,0:T(8,128)}, u32[]{:S(2)}) copy-start(f32[128,128]{1,0:T(8,128)} %copy-done.19) | copy-start | bytes 196612
  144.6 74.0 %all-gather.13.cloned.1.call-start = ((), (), s32[]{:S(2)}) async-start(), calls=%async_computation.2 | async-start | bytes 1310720 | tf_op jit(solution)/shard_map/all_gather | solution.py:105
  172.6 148.1 %all-gather.15.cloned.1.call-start = ((), (), s32[]{:S(2)}) async-start(), calls=%async_computation.3 | async-start | bytes 8650752 | tf_op jit(solution)/shard_map/all_gather | solution.py:21
  175.2 1.1 copy-start.11
  175.2 1.1 copy-start.22
  176.3 1.5 copy-start.2
  178.9 1.4 copy-start.1
  223.4 9.0 %copy-start.3 = (f32[1792,256]{1,0:T(8,128)S(1)}, f32[1792,256]{1,0:T(8,128)}, u32[]{:S(2)}) copy-start(f32[1792,256]{1,0:T(8,128)} %fusion.31) | copy-start | bytes 5505028
  232.4 2.2 copy-start.4
  238.4 15.7 %copy-start.8 = (f32[4,256,1,256]{3,1,2,0:T(8,128)S(1)}, f32[4,256,1,256]{3,1,2,0:T(8,128)}, u32[]{:S(2)}) copy-start(f32[4,256,1,256]{3,1,2,0:T(8,128)} %all-gather.13.cloned.1.call-done) | copy-start | bytes 3145732
  238.6 0.7 copy-start.15
  253.0 2.2 copy-start.14
  255.2 5.6 %copy-start.16 = (f32[256,256]{0,1:T(8,128)S(1)}, f32[256,256]{0,1:T(8,128)}, u32[]{:S(2)}) copy-start(f32[256,256]{0,1:T(8,128)} %copy-done.15) | copy-start | bytes 786436
  278.9 1.9 copy-start.5
  363.4 2.3 copy-start.13
  384.8 2.6 copy-start.9
  403.1 2.0 copy-start.12
Sparse Core Ops, SparseCore 0:
  11.3 80.1 all-gather.8
  144.7 26.5 all-gather.10
  172.9 27.4 all-gather.12
  223.5 76.3 all-gather.14

commit v7 on v5

--- a/solution.py
+++ b/solution.py
@@ -14,20 +14,19 @@
     sep_slots, tile, cslots, _ = sep_local.shape
     if sep_slots == 1 and n_row == n_columns:
         pieces = []
+        previous = None
         for t in range(cslots):
-            piece = sep_local[0, :, t, :]
-            if t == 1:
-                piece = piece + after_first(pieces[0])
+            piece = sep_local[0, :, t, :] + after_first(t, previous)
             pieces.append(lax.all_gather(piece, ("col", "row"), axis=0))
-        if cslots == 1:
-            after_first(pieces[0])
+            previous = after(pieces[-1])
 
         def panel(k):
             base = (k % n_col) * n_row
             return pieces[k // n_col][base + k:base + n_row].reshape((n_columns - k) * tile, tile)
 
         return panel
-    after_first(None)
+    for t in range(cslots):
+        after_first(t, None)
     g = lax.all_gather(sep_local, "row", axis=1, tiled=True)
     g = g.reshape(sep_slots * n_row * tile, cslots, tile)[: n_columns * tile]
     g = lax.all_gather(g, "col", axis=2)
@@ -93,16 +92,12 @@
     tail_first = n_columns // n_row
     n_tail = (slot_count - tail_first) * tile
     tail_pieces = []
-    tail_sources = []
 
-    def gather_tail(first_piece):
-        tail_local = working[tail_first:]
-        if first_piece is not None:
-            tail_local = tail_local + after(first_piece)
-        tail_sources.append(tail_local)
-        for t in range(col_slot_count):
-            piece = tail_local[:, :, t, :].reshape(n_tail, tile)
-            tail_pieces.append(lax.all_gather(piece, "col", axis=0))
+    def gather_tail(t, dependency):
+        piece = working[tail_first:, :, t, :].reshape(n_tail, tile)
+        if dependency is not None:
+            piece = piece + dependency
+        tail_pieces.append(lax.all_gather(piece, "col", axis=0))
         return after(tail_pieces[-1])
 
     sep_slots = -(-n_columns // n_row)
@@ -118,8 +113,6 @@
             top = factor[k * tile:(k + 1) * tile, : k * tile]
             panel = panel - mm(left, top.T, lax.Precision.HIGH)
         diag = panel[:tile]
-        if k == 0:
-            diag = diag + after(tail_sources[0])
         diag = jnp.tril(diag) + jnp.tril(diag, -1).T
         lkk, linv = factor_diag(diag)
         below = mm(panel[tile:], linv.T)

time: 525 us -> 554 us (1.055)
  waiting for transfers between devices: 90 us -> 113 us
  local copies, waits for them, and re-layouts: 79.1 us -> 86.4 us
  other arithmetic: 245 us -> 239 us
    all_gather x2, waiting for transfers between devices: 10.3 us -> 30.7 us  [gather_tail(): tail_pieces.append(lax.all_gather(piece, 'col', axis=0))]
    another operation x24, other arithmetic: 108 us -> 101 us  [factor_diag(): l11 = jnp.tril(lax.linalg.cholesky(s11, symmetrize_input=True))]
    unnamed x57 -> x69, local copies, waits for them, and re-layouts: 21.1 us -> 24.9 us
  transfers between devices with their start and end apart: 4 -> 4, of which waited for: 2 -> 3; matrix products, arithmetic and copies ran while one was open for 32% -> 18% of each run, Pallas kernels for 0% -> 0%
where the time goes in v7:
time: 554 us; the launch traced here: 543 us
  other arithmetic  239 us (43%)
  waiting for transfers between devices  113 us (20%)
  local copies, waits for them, and re-layouts  86.4 us (16%)
  matrix products  86 us (16%)
  between operations  18.5 us (3%)
    another operation x24, other arithmetic, factor_diag(): l11 = jnp.tril(lax.linalg.cholesky(s11, symmetrize_input=True))  101 us
    another operation x24, other arithmetic, factor_diag(): lax.linalg.cholesky(diag[:half, :half], symmetrize_input=False)  101 us
    dot_general x159, matrix products, mm(): jnp.dot(a, b, precision=precision, preferred_element_type=jnp.float32)  86 us
    all_gather x2, waiting for transfers between devices, separator_panels(): pieces.append(lax.all_gather(piece, ('col', 'row'), axis=0))  82.5 us
    all_gather x2, waiting for transfers between devices, gather_tail(): tail_pieces.append(lax.all_gather(piece, 'col', axis=0))  30.7 us
    unnamed x69, local copies, waits for them, and re-layouts  24.9 us
    slice x8, local copies, waits for them, and re-layouts, panel(): pieces[k // n_col][base + k:base + n_row]  15.4 us
    reduce_sum x16, other arithmetic, lower_inverse(): diag = jnp.sum(lower * eye, axis=1)  11.5 us
  transfers between devices with their start and end apart: 4, of which 3 were waited for; matrix products, arithmetic and copies ran while one was open for 18% of the time, Pallas kernels for 0%

profile of v7, /device:TPU:0, one launch (start us, length us, event | category | flops | bytes accessed | tf_op | source)
XLA Modules:
  0.0 543.3 jit_solution(15138166035116925619)
XLA Ops:
  10.3 30.7 %all-gather.9.cloned.1.call-done = f32[4,256,1,256]{3,1,2,0:T(8,128)} async-done(((f32[1,256,1,256]{3,1,2,0:T(8,128)}), f32[4,256,1,256]{3,1,2,0:T(8,128)}) %all-gather.9.cloned.1.call-update) | async-done | bytes 1048592 | tf_op jit(solution)/shard_map/all_gather | solution.py:100
  41.0 1.9 copy.406
  48.8 73.1 %all-gather.11.cloned.1.call-done = f32[32,256,1,256]{3,1,2,0:T(8,128)} async-done(((f32[1,256,1,256]{3,1,2,0:T(8,128)}), f32[32,256,1,256]{3,1,2,0:T(8,128)}) %all-gather.11.cloned.1.call-update) | async-done | bytes 8388624 | tf_op jit(solution)/shard_map/all_gather | solution.py:20
  124.1 11.7 %custom-call.18 = f32[128,128]{1,0:T(8,128)S(1)} custom-call(f32[128,128]{1,0:T(8,128)S(1)} %copy.213), custom_call_target="Cholesky" | custom-call | tf_op jit(solution)/shard_map/cholesky/custom-call.1 | solution.py:62
  141.6 2.5 slice.1447
  144.1 2.8 slice.1414
  146.9 2.9 slice.1381
  149.8 1.8 slice.1367
  151.9 11.7 %custom-call.19 = f32[128,128]{1,0:T(8,128)S(1)} custom-call(f32[128,128]{1,0:T(8,128)S(1)} %copy.217), custom_call_target="Cholesky" | custom-call | tf_op jit(solution)/shard_map/cholesky/custom-call.1 | solution.py:66
  167.8 2.8 copy.224
  171.9 2.9 fusion.26
  179.5 1.8 copy.227
  183.9 12.5 %custom-call.20 = f32[128,128]{1,0:T(8,128)S(1)} custom-call(f32[128,128]{1,0:T(8,128)} %copy.228), custom_call_target="Cholesky" | custom-call | tf_op jit(solution)/shard_map/cholesky/custom-call.1 | solution.py:62
  202.7 2.8 copy.252
  205.5 3.1 copy.238
  210.7 1.6 copy.232
  212.3 12.9 %custom-call.21 = f32[128,128]{1,0:T(8,128)S(1)} custom-call(f32[128,128]{1,0:T(8,128)} %copy.232), custom_call_target="Cholesky" | custom-call | tf_op jit(solution)/shard_map/cholesky/custom-call.1 | solution.py:66
  229.4 4.2 fusion.31
  233.7 12.2 %copy.407 = f32[1024,2,8,128]{3,1,2,0:T(2,128)S(1)} copy(f32[1024,2,8,128]{3,2,1,0:T(8,128)} %bitcast.161) | data formatting | bytes 16777216
  248.0 9.0 %scatter.26 = f32[2304,2048]{1,0:T(8,128)} pad(f32[2304,256]{1,0:T(8,128)S(1)} %fusion.22, f32[]{:T(128)} %constant.352.clone.1), padding=0_0x0_1792 | pad | bytes 21233668 | tf_op jit(solution)/shard_map/scatter | solution.py:119
  259.2 3.8 fusion.18
  263.4 11.7 %custom-call.22 = f32[128,128]{1,0:T(8,128)S(1)} custom-call(f32[128,128]{1,0:T(8,128)S(1)} %copy.242), custom_call_target="Cholesky" | custom-call | tf_op jit(solution)/shard_map/cholesky/custom-call.1 | solution.py:62
  278.8 1.8 copy.408
  284.7 11.9 %custom-call.23 = f32[128,128]{1,0:T(8,128)S(1)} custom-call(f32[128,128]{1,0:T(8,128)S(1)} %copy.246), custom_call_target="Cholesky" | custom-call | tf_op jit(solution)/shard_map/cholesky/custom-call.1 | solution.py:66
  300.6 2.7 fusion.36
  305.3 4.8 fusion.15
  310.5 12.1 %custom-call.24 = f32[128,128]{1,0:T(8,128)S(1)} custom-call(f32[128,128]{1,0:T(8,128)S(1)} %copy.256), custom_call_target="Cholesky" | custom-call | tf_op jit(solution)/shard_map/cholesky/custom-call.1 | solution.py:62
  327.1 11.7 %custom-call.25 = f32[128,128]{1,0:T(8,128)S(1)} custom-call(f32[128,128]{1,0:T(8,128)S(1)} %copy.260), custom_call_target="Cholesky" | custom-call | tf_op jit(solution)/shard_map/cholesky/custom-call.1 | solution.py:66
  342.9 2.3 fusion.44
  349.5 9.4 %all-gather.15.cloned.1.call-done = f32[32,256,1,256]{3,1,2,0:T(8,128)} async-done(((f32[1,256,1,256]{3,1,2,0:T(8,128)}), f32[32,256,1,256]{3,1,2,0:T(8,128)}) %all-gather.15.cloned.1.call-update) | async-done | bytes 8388624 | tf_op jit(solution)/shard_map/all_gather | solution.py:20
  358.8 1.9 slice.1550
  363.5 5.2 fusion.12
  369.2 11.7 %custom-call.26 = f32[128,128]{1,0:T(8,128)S(1)} custom-call(f32[128,128]{1,0:T(8,128)S(1)} %copy.270), custom_call_target="Cholesky" | custom-call | tf_op jit(solution)/shard_map/cholesky/custom-call.1 | solution.py:62
  385.7 11.7 %custom-call.27 = f32[128,128]{1,0:T(8,128)S(1)} custom-call(f32[128,128]{1,0:T(8,128)S(1)} %copy.274), custom_call_target="Cholesky" | custom-call | tf_op jit(solution)/shard_map/cholesky/custom-call.1 | solution.py:66
  401.5 1.8 fusion.58
  404.5 5.1 fusion.38
  410.0 11.7 %custom-call.28 = f32[128,128]{1,0:T(8,128)S(1)} custom-call(f32[128,128]{1,0:T(8,128)S(1)} %copy.281), custom_call_target="Cholesky" | custom-call | tf_op jit(solution)/shard_map/cholesky/custom-call.1 | solution.py:62
  426.5 12.1 %custom-call.29 = f32[128,128]{1,0:T(8,128)S(1)} custom-call(f32[128,128]{1,0:T(8,128)S(1)} %copy.285), custom_call_target="Cholesky" | custom-call | tf_op jit(solution)/shard_map/cholesky/custom-call.1 | solution.py:66
  444.5 4.9 fusion.46
  449.7 11.7 %custom-call.30 = f32[128,128]{1,0:T(8,128)S(1)} custom-call(f32[128,128]{1,0:T(8,128)S(1)} %copy.295), custom_call_target="Cholesky" | custom-call | tf_op jit(solution)/shard_map/cholesky/custom-call.1 | solution.py:62
  467.3 11.7 %custom-call.31 = f32[128,128]{1,0:T(8,128)S(1)} custom-call(f32[128,128]{1,0:T(8,128)S(1)} %fusion.510), custom_call_target="Cholesky" | custom-call | tf_op jit(solution)/shard_map/cholesky/custom-call.1 | solution.py:66
  484.9 4.2 fusion.51
  489.5 11.9 %custom-call.32 = f32[128,128]{1,0:T(8,128)S(1)} custom-call(f32[128,128]{1,0:T(8,128)S(1)} %copy.306), custom_call_target="Cholesky" | custom-call | tf_op jit(solution)/shard_map/cholesky/custom-call.1 | solution.py:62
  506.2 11.7 %custom-call.33 = f32[128,128]{1,0:T(8,128)S(1)} custom-call(f32[128,128]{1,0:T(8,128)S(1)} %broadcast_multiply_fusion.1), custom_call_target="Cholesky" | custom-call | tf_op jit(solution)/shard_map/cholesky/custom-call.1 | solution.py:66
  523.2 3.9 constant_dynamic-slice_fusion.3
  527.2 2.9 copy.313
  531.4 1.8 copy.315
  534.6 1.8 copy.317
  (489 shorter events, 119.8 us)
Async XLA Ops:
  6.5 34.5 %all-gather.9.cloned.1.call-start = ((), (), s32[]{:S(2)}) async-start(), calls=%async_computation | async-start | bytes 1310720 | tf_op jit(solution)/shard_map/all_gather | solution.py:100
  10.2 111.7 %all-gather.11.cloned.1.call-start = ((), (), s32[]{:S(2)}) async-start(), calls=%async_computation.1 | async-start | bytes 8650752 | tf_op jit(solution)/shard_map/all_gather | solution.py:20
  41.0 4.5 copy-start.7
  44.8 234.0 %all-gather.13.cloned.1.call-start = ((), (), s32[]{:S(2)}) async-start(), calls=%async_computation.2 | async-start | bytes 1310720 | tf_op jit(solution)/shard_map/all_gather | solution.py:100
  165.0 5.6 %copy-start.13 = (f32[128,128]{1,0:T(8,128)}, f32[128,128]{1,0:T(8,128)S(1)}, u32[]{:S(2)}) copy-start(f32[128,128]{1,0:T(8,128)S(1)} %get-tuple-element.131) | copy-start | bytes 196612
  167.8 3.9 copy-start.27
  171.9 2.9 copy-start.14
  171.9 2.9 copy-start.26
  174.9 1.5 copy-start.2
  174.9 1.5 copy-start.18
  177.4 1.4 copy-start
  182.5 0.7 copy-start.20
  196.4 3.5 copy-start.21
  197.7 3.3 copy-start.9
  199.9 1.1 copy-start.22
  205.5 3.1 copy-start.24
  225.3 3.9 copy-start.28
  226.7 0.6 copy-start.11
  226.8 2.6 copy-start.1
  226.8 2.6 copy-start.23
  247.7 9.2 %copy-start.10 = (f32[128,128]{1,0:T(8,128)S(1)}, f32[128,128]{1,0:T(8,128)}, u32[]{:S(2)}) copy-start(f32[128,128]{1,0:T(8,128)} %copy-done.9) | copy-start | bytes 196612
  247.7 111.1 %all-gather.15.cloned.1.call-start = ((), (), s32[]{:S(2)}) async-start(), calls=%async_computation.3 | async-start | bytes 8650752 | tf_op jit(solution)/shard_map/all_gather | solution.py:20
  248.0 9.0 %copy-start.3 = (f32[1792,256]{1,0:T(8,128)S(1)}, f32[1792,256]{1,0:T(8,128)}, u32[]{:S(2)}) copy-start(f32[1792,256]{1,0:T(8,128)} %fusion.31) | copy-start | bytes 5505028
  248.0 9.0 %copy-start.12 = (f32[128,128]{1,0:T(8,128)S(1)}, f32[128,128]{1,0:T(8,128)}, u32[]{:S(2)}) copy-start(f32[128,128]{1,0:T(8,128)} %copy-done.11) | copy-start | bytes 196612
  248.0 9.0 %copy-start.25 = (f32[128,128]{1,0:T(8,128)S(1)}, f32[128,128]{1,0:T(8,128)}, u32[]{:S(2)}) copy-start(f32[128,128]{1,0:T(8,128)} %copy.233) | copy-start | bytes 196612
  257.0 2.2 copy-start.4
  257.0 2.2 copy-start.16
  303.3 1.9 copy-start.5
  303.3 2.0 copy-start.15
  345.2 1.7 copy-start.6
  401.4 3.0 copy-start.19
  423.5 2.6 copy-start.8
  442.0 2.4 copy-start.17
Sparse Core Ops, SparseCore 0:
  10.3 30.6 all-gather.8
  44.9 76.9 all-gather.10
  247.8 26.5 all-gather.12
  282.6 76.2 all-gather.14

commit v8 on v5

--- a/solution.py
+++ b/solution.py
@@ -112,7 +112,10 @@
     factor = jnp.zeros((total_rows, n_columns * tile), jnp.float32)
     for k in range(n_columns):
         cols = slice(k * tile, (k + 1) * tile)
-        panel = jnp.concatenate([get_panel(k), tail_pieces[k // n_col][k % n_col]], axis=0)
+        if k == 0:
+            panel = get_panel(k)
+        else:
+            panel = jnp.concatenate([get_panel(k), tail_pieces[k // n_col][k % n_col]], axis=0)
         if k > 0:
             left = factor[k * tile:, : k * tile]
             top = factor[k * tile:(k + 1) * tile, : k * tile]
@@ -123,7 +126,12 @@
         diag = jnp.tril(diag) + jnp.tril(diag, -1).T
         lkk, linv = factor_diag(diag)
         below = mm(panel[tile:], linv.T)
-        factor = factor.at[k * tile:, cols].set(jnp.concatenate([lkk, below], axis=0))
+        if k == 0:
+            factor = lax.dynamic_update_slice(factor, jnp.concatenate([lkk, below], axis=0), (0, 0))
+            tail_below = mm(tail_pieces[0][0], linv.T)
+            factor = lax.dynamic_update_slice(factor, tail_below, (n_columns * tile, 0))
+        else:
+            factor = factor.at[k * tile:, cols].set(jnp.concatenate([lkk, below], axis=0))
 
     outs = []
     for slot in range(slot_count):

time: 525 us -> 516 us (0.983)
  waiting for transfers between devices: 90 us -> 84.7 us
    scatter x1 -> x0, local copies, waits for them, and re-layouts: 8.98 us -> none  [shards(): factor.at[k * tile:, cols].set(jnp.concatenate([lkk, below], axis=0))]
    dynamic_update_slice x0 -> x1, local copies, waits for them, and re-layouts: none -> 8.93 us  [shards(): lax.dynamic_update_slice(factor, jnp.concatenate([lkk, below], axis=0), (...]
    all_gather x2, waiting for transfers between devices: 10.3 us -> 4.4 us  [gather_tail(): tail_pieces.append(lax.all_gather(piece, 'col', axis=0))]
    unnamed x57 -> x53, local copies, waits for them, and re-layouts: 21.1 us -> 19.1 us
    dot_general x159 -> x160, matrix products: 83.9 us -> 85.1 us  [mm(): jnp.dot(a, b, precision=precision, preferred_element_type=jnp.float32)]
    slice x8 -> x7, local copies, waits for them, and re-layouts: 13 us -> 13.4 us  [panel(): pieces[k // n_col][base + k:base + n_row]]
  transfers between devices with their start and end apart: 4 -> 4, of which waited for: 2 -> 2; matrix products, arithmetic and copies ran while one was open for 32% -> 33% of each run, Pallas kernels for 0% -> 0%
where the time goes in v8:
time: 516 us; the launch traced here: 508 us
  other arithmetic  243 us (47%)
  matrix products  85.1 us (16%)
  waiting for transfers between devices  84.7 us (16%)
  local copies, waits for them, and re-layouts  76 us (15%)
  between operations  18.6 us (4%)
    another operation x24, other arithmetic, factor_diag(): l11 = jnp.tril(lax.linalg.cholesky(s11, symmetrize_input=True))  109 us
    another operation x24, other arithmetic, factor_diag(): lax.linalg.cholesky(diag[:half, :half], symmetrize_input=False)  101 us
    dot_general x160, matrix products, mm(): jnp.dot(a, b, precision=precision, preferred_element_type=jnp.float32)  85.1 us
    all_gather x2, waiting for transfers between devices, separator_panels(): pieces.append(lax.all_gather(piece, ('col', 'row'), axis=0))  80.2 us
    unnamed x53, local copies, waits for them, and re-layouts  19.1 us
    slice x7, local copies, waits for them, and re-layouts, panel(): pieces[k // n_col][base + k:base + n_row]  13.4 us
    reduce_sum x16, other arithmetic, lower_inverse(): diag = jnp.sum(lower * eye, axis=1)  12.1 us
  transfers between devices with their start and end apart: 4, of which 2 were waited for; matrix products, arithmetic and copies ran while one was open for 33% of the time, Pallas kernels for 0%

profile of v8, /device:TPU:0, one launch (start us, length us, event | category | flops | bytes accessed | tf_op | source)
XLA Modules:
  0.0 507.9 jit_solution(8992700245046224121)
XLA Ops:
  11.3 80.2 %all-gather.9.cloned.1.call-done = f32[32,256,1,256]{3,1,2,0:T(8,128)} async-done(((f32[1,256,1,256]{3,1,2,0:T(8,128)}), f32[32,256,1,256]{3,1,2,0:T(8,128)}) %all-gather.9.cloned.1.call-update) | async-done | bytes 8388624 | tf_op jit(solution)/shard_map/all_gather | solution.py:21
  91.5 2.5 slice.1434
  95.7 3.9 fusion.684
  99.6 4.8 copy.521
  108.5 1.8 copy.464
  114.6 1.8 copy.326
  118.9 12.5 %custom-call.18 = f32[128,128]{1,0:T(8,128)S(1)} custom-call(f32[128,128]{1,0:T(8,128)} %copy.327), custom_call_target="Cholesky" | custom-call | tf_op jit(solution)/shard_map/cholesky/custom-call.1 | solution.py:63
  137.6 2.8 copy.367
  142.0 1.7 copy.339
  144.3 11.7 %custom-call.19 = f32[128,128]{1,0:T(8,128)S(1)} custom-call(f32[128,128]{1,0:T(8,128)S(1)} %copy.331), custom_call_target="Cholesky" | custom-call | tf_op jit(solution)/shard_map/cholesky/custom-call.1 | solution.py:67
  162.1 8.9 %dynamic_update_slice.6 = f32[2304,2048]{1,0:T(8,128)} pad(f32[2048,256]{1,0:T(8,128)S(1)} %fusion.24, f32[]{:T(128)} %constant.324.clone.1), padding=0_256x0_1792 | pad | bytes 20971524 | tf_op jit(solution)/shard_map/dynamic_update_slice | solution.py:130
  171.0 1.8 fusion.686
  173.1 2.1 convolution_dynamic-update-slice_fusion
  175.2 3.3 convolution_subtract_fusion
  178.9 11.7 %custom-call.20 = f32[128,128]{1,0:T(8,128)S(1)} custom-call(f32[128,128]{1,0:T(8,128)S(1)} %copy.343), custom_call_target="Cholesky" | custom-call | tf_op jit(solution)/shard_map/cholesky/custom-call.1 | solution.py:63
  195.1 4.4 all-gather.13.cloned.1.call-done
  199.5 1.8 copy.523
  202.5 1.7 slice_add_fusion.1
  204.4 20.4 %custom-call.21 = f32[128,128]{1,0:T(8,128)S(1)} custom-call(f32[128,128]{1,0:T(8,128)S(1)} %copy.347), custom_call_target="Cholesky" | custom-call | tf_op jit(solution)/shard_map/cholesky/custom-call.1 | solution.py:67
  228.6 3.1 fusion.28
  233.9 3.9 fusion.18
  238.9 11.9 %custom-call.22 = f32[128,128]{1,0:T(8,128)S(1)} custom-call(f32[128,128]{1,0:T(8,128)S(1)} %copy.357), custom_call_target="Cholesky" | custom-call | tf_op jit(solution)/shard_map/cholesky/custom-call.1 | solution.py:63
  256.0 1.8 copy.469
  257.8 1.8 copy.468
  261.2 11.7 %custom-call.23 = f32[128,128]{1,0:T(8,128)S(1)} custom-call(f32[128,128]{1,0:T(8,128)S(1)} %copy.361), custom_call_target="Cholesky" | custom-call | tf_op jit(solution)/shard_map/cholesky/custom-call.1 | solution.py:67
  277.1 3.1 fusion.33
  282.1 4.7 fusion.15
  287.2 11.7 %custom-call.24 = f32[128,128]{1,0:T(8,128)S(1)} custom-call(f32[128,128]{1,0:T(8,128)S(1)} %copy.371), custom_call_target="Cholesky" | custom-call | tf_op jit(solution)/shard_map/cholesky/custom-call.1 | solution.py:63
  303.3 11.9 %custom-call.25 = f32[128,128]{1,0:T(8,128)S(1)} custom-call(f32[128,128]{1,0:T(8,128)S(1)} %copy.375), custom_call_target="Cholesky" | custom-call | tf_op jit(solution)/shard_map/cholesky/custom-call.1 | solution.py:67
  319.3 2.3 fusion.41
  322.9 1.9 slice.1536
  327.6 5.0 fusion.12
  333.1 11.7 %custom-call.26 = f32[128,128]{1,0:T(8,128)S(1)} custom-call(f32[128,128]{1,0:T(8,128)S(1)} %copy.385), custom_call_target="Cholesky" | custom-call | tf_op jit(solution)/shard_map/cholesky/custom-call.1 | solution.py:63
  349.9 11.7 %custom-call.27 = f32[128,128]{1,0:T(8,128)S(1)} custom-call(f32[128,128]{1,0:T(8,128)S(1)} %copy.389), custom_call_target="Cholesky" | custom-call | tf_op jit(solution)/shard_map/cholesky/custom-call.1 | solution.py:67
  365.5 1.8 fusion.55
  368.6 5.1 %fusion.35 = f32[1024,256]{1,0:T(8,128)S(1)} fusion(f32[2304,2048]{1,0:T(8,128)} %fusion.40, f32[256,256]{1,0:T(8,128)S(1)} %copy-done.14, f32[768,256]{1,0:T(8,128)S(1)} %bitcast.165), kind=kOutput, calls=%fused_computation.149 | convolution fusion | flops 2013790208 | bytes 8650752 | tf_op jit(solution)/shard_map/dot_general | solution.py:10
  374.1 12.1 %custom-call.28 = f32[128,128]{1,0:T(8,128)S(1)} custom-call(f32[128,128]{1,0:T(8,128)S(1)} %copy.396), custom_call_target="Cholesky" | custom-call | tf_op jit(solution)/shard_map/cholesky/custom-call.1 | solution.py:63
  391.3 11.7 %custom-call.29 = f32[128,128]{1,0:T(8,128)S(1)} custom-call(f32[128,128]{1,0:T(8,128)S(1)} %copy.400), custom_call_target="Cholesky" | custom-call | tf_op jit(solution)/shard_map/cholesky/custom-call.1 | solution.py:67
  408.8 5.0 fusion.43
  414.2 11.7 %custom-call.30 = f32[128,128]{1,0:T(8,128)S(1)} custom-call(f32[128,128]{1,0:T(8,128)S(1)} %copy.410), custom_call_target="Cholesky" | custom-call | tf_op jit(solution)/shard_map/cholesky/custom-call.1 | solution.py:63
  431.7 11.7 %custom-call.31 = f32[128,128]{1,0:T(8,128)S(1)} custom-call(f32[128,128]{1,0:T(8,128)S(1)} %fusion.504), custom_call_target="Cholesky" | custom-call | tf_op jit(solution)/shard_map/cholesky/custom-call.1 | solution.py:67
  449.4 4.2 fusion.48
  454.0 11.7 %custom-call.32 = f32[128,128]{1,0:T(8,128)S(1)} custom-call(f32[128,128]{1,0:T(8,128)S(1)} %copy.421), custom_call_target="Cholesky" | custom-call | tf_op jit(solution)/shard_map/cholesky/custom-call.1 | solution.py:63
  470.5 11.9 %custom-call.33 = f32[128,128]{1,0:T(8,128)S(1)} custom-call(f32[128,128]{1,0:T(8,128)S(1)} %broadcast_multiply_fusion.1), custom_call_target="Cholesky" | custom-call | tf_op jit(solution)/shard_map/cholesky/custom-call.1 | solution.py:67
  487.8 3.9 constant_dynamic-slice_fusion.3
  491.7 2.9 copy.428
  495.9 1.9 copy.430
  499.1 1.8 copy.432
  (475 shorter events, 113.5 us)
Async XLA Ops:
  6.5 85.0 %all-gather.9.cloned.1.call-start = ((), (), s32[]{:S(2)}) async-start(), calls=%async_computation | async-start | bytes 8650752 | tf_op jit(solution)/shard_map/all_gather | solution.py:21
  9.5 1.0 copy-start.4
  11.2 159.8 %all-gather.11.cloned.1.call-start = ((), (), s32[]{:S(2)}) async-start(), calls=%async_computation.1 | async-start | bytes 1310720 | tf_op jit(solution)/shard_map/all_gather | solution.py:105
  94.0 5.6 %copy-start = (f32[32,256,1,256]{3,1,2,0:T(8,128)S(1)}, f32[32,256,1,256]{3,1,2,0:T(8,128)}, u32[]{:S(2)}) copy-start(f32[32,256,1,256]{3,1,2,0:T(8,128)} %all-gather.9.cloned.1.call-done) | copy-start | bytes 25165828
  99.6 6.1 %copy-start.5 = (f32[2,256,2,256]{3,1,2,0:T(8,128)S(1)}, f32[2,256,2,256]{3,1,2,0:T(8,128)}, u32[]{:S(2)}) copy-start(f32[2,256,2,256]{3,1,2,0:T(8,128)} %copy-done.4) | copy-start | bytes 3145732
  117.5 0.7 copy-start.17
  131.5 4.3 copy-start.18
  132.9 2.0 copy-start.8
  135.1 0.6 copy-start.10
  142.0 2.0 copy-start.19
  143.7 14.8 %copy-start.11 = (f32[128,128]{1,0:T(8,128)S(1)}, f32[128,128]{1,0:T(8,128)}, u32[]{:S(2)}) copy-start(f32[128,128]{1,0:T(8,128)} %copy-done.10) | copy-start | bytes 196612
  143.8 55.8 %all-gather.13.cloned.1.call-start = ((), (), s32[]{:S(2)}) async-start(), calls=%async_computation.2 | async-start | bytes 1310720 | tf_op jit(solution)/shard_map/all_gather | solution.py:105
  157.9 2.4 copy-start.1
  159.8 163.1 %all-gather.15.cloned.1.call-start = ((), (), s32[]{:S(2)}) async-start(), calls=%async_computation.3 | async-start | bytes 8650752 | tf_op jit(solution)/shard_map/all_gather | solution.py:21
  160.0 1.9 copy-start.9
  160.1 1.9 copy-start.20
  231.8 2.2 copy-start.2
  237.8 15.9 %copy-start.6 = (f32[4,256,1,256]{3,1,2,0:T(8,128)S(1)}, f32[4,256,1,256]{3,1,2,0:T(8,128)}, u32[]{:S(2)}) copy-start(f32[4,256,1,256]{3,1,2,0:T(8,128)} %all-gather.13.cloned.1.call-done) | copy-start | bytes 3145732
  238.1 0.7 copy-start.15
  252.8 2.0 copy-start.13
  254.7 5.7 %copy-start.16 = (f32[256,256]{0,1:T(8,128)S(1)}, f32[256,256]{0,1:T(8,128)}, u32[]{:S(2)}) copy-start(f32[256,256]{0,1:T(8,128)} %copy-done.15) | copy-start | bytes 786436
  280.2 1.9 copy-start.3
  365.5 3.0 copy-start.14
  388.2 2.6 copy-start.7
  406.4 2.4 copy-start.12
Sparse Core Ops, SparseCore 0:
  11.3 80.1 all-gather.8
  143.9 26.5 all-gather.10
  172.0 27.4 all-gather.12
  204.3 76.8 all-gather.14

commit v9 on v8

--- a/solution.py
+++ b/solution.py
@@ -103,7 +103,7 @@
         for t in range(col_slot_count):
             piece = tail_local[:, :, t, :].reshape(n_tail, tile)
             tail_pieces.append(lax.all_gather(piece, "col", axis=0))
-        return after(tail_pieces[-1])
+        return after(tail_pieces[0])
 
     sep_slots = -(-n_columns // n_row)
     get_panel = separator_panels(working[:sep_slots], n_row, n_col, n_columns, gather_tail)

time: 516 us -> 522 us (1.012)
    all_gather x2, waiting for transfers between devices: 80.2 us -> 88 us  [separator_panels(): pieces.append(lax.all_gather(piece, ('col', 'row'), axis=0))]
    unnamed x53 -> x61, local copies, waits for them, and re-layouts: 19.1 us -> 17.4 us
  transfers between devices with their start and end apart: 4 -> 4, of which waited for: 2 -> 2; matrix products, arithmetic and copies ran while one was open for 33% -> 34% of each run, Pallas kernels for 0% -> 0%
where the time goes in v9:
time: 522 us; the launch traced here: 514 us
  other arithmetic  243 us (47%)
  waiting for transfers between devices  88.1 us (17%)
  matrix products  86.1 us (16%)
  local copies, waits for them, and re-layouts  77.9 us (15%)
  between operations  18.6 us (4%)
    another operation x24, other arithmetic, factor_diag(): l11 = jnp.tril(lax.linalg.cholesky(s11, symmetrize_input=True))  109 us
    another operation x24, other arithmetic, factor_diag(): lax.linalg.cholesky(diag[:half, :half], symmetrize_input=False)  101 us
    all_gather x2, waiting for transfers between devices, separator_panels(): pieces.append(lax.all_gather(piece, ('col', 'row'), axis=0))  88 us
    dot_general x160, matrix products, mm(): jnp.dot(a, b, precision=precision, preferred_element_type=jnp.float32)  86.1 us
    unnamed x61, local copies, waits for them, and re-layouts  17.4 us
    slice x7, local copies, waits for them, and re-layouts, panel(): pieces[k // n_col][base + k:base + n_row]  13.5 us
    reduce_sum x16, other arithmetic, lower_inverse(): diag = jnp.sum(lower * eye, axis=1)  11.9 us
  transfers between devices with their start and end apart: 4, of which 2 were waited for; matrix products, arithmetic and copies ran while one was open for 34% of the time, Pallas kernels for 0%

profile of v9, /device:TPU:0, one launch (start us, length us, event | category | flops | bytes accessed | tf_op | source)
XLA Modules:
  0.0 514.2 jit_solution(18399940041748248027)
XLA Ops:
  11.3 80.2 %all-gather.9.cloned.1.call-done = f32[32,256,1,256]{3,1,2,0:T(8,128)} async-done(((f32[1,256,1,256]{3,1,2,0:T(8,128)}), f32[32,256,1,256]{3,1,2,0:T(8,128)}) %all-gather.9.cloned.1.call-update) | async-done | bytes 8388624 | tf_op jit(solution)/shard_map/all_gather | solution.py:21
  91.5 2.5 slice.1434
  94.0 1.7 slice.1401
  95.7 4.0 fusion.684
  99.7 4.8 copy.521
  108.5 1.8 copy.464
  112.9 1.7 add_bitcast_fusion
  114.5 1.8 copy.326
  118.9 12.5 %custom-call.18 = f32[128,128]{1,0:T(8,128)S(1)} custom-call(f32[128,128]{1,0:T(8,128)} %copy.327), custom_call_target="Cholesky" | custom-call | tf_op jit(solution)/shard_map/cholesky/custom-call.1 | solution.py:63
  137.6 2.8 copy.367
  142.1 1.7 copy.339
  144.3 11.7 %custom-call.19 = f32[128,128]{1,0:T(8,128)S(1)} custom-call(f32[128,128]{1,0:T(8,128)S(1)} %copy.331), custom_call_target="Cholesky" | custom-call | tf_op jit(solution)/shard_map/cholesky/custom-call.1 | solution.py:67
  162.1 8.9 %dynamic_update_slice.6 = f32[2304,2048]{1,0:T(8,128)} pad(f32[2048,256]{1,0:T(8,128)S(1)} %fusion.24, f32[]{:T(128)} %constant.324.clone.1), padding=0_256x0_1792 | pad | bytes 20971524 | tf_op jit(solution)/shard_map/dynamic_update_slice | solution.py:130
  171.0 2.0 fusion.686
  174.4 3.3 convolution_subtract_fusion
  180.4 11.7 %custom-call.20 = f32[128,128]{1,0:T(8,128)S(1)} custom-call(f32[128,128]{1,0:T(8,128)S(1)} %copy.343), custom_call_target="Cholesky" | custom-call | tf_op jit(solution)/shard_map/cholesky/custom-call.1 | solution.py:63
  198.0 1.8 copy.466
  201.8 20.4 %custom-call.21 = f32[128,128]{1,0:T(8,128)S(1)} custom-call(f32[128,128]{1,0:T(8,128)S(1)} %copy.347), custom_call_target="Cholesky" | custom-call | tf_op jit(solution)/shard_map/cholesky/custom-call.1 | solution.py:67
  226.2 3.1 fusion.28
  231.5 3.9 fusion.18
  236.4 11.9 %custom-call.22 = f32[128,128]{1,0:T(8,128)S(1)} custom-call(f32[128,128]{1,0:T(8,128)S(1)} %copy.357), custom_call_target="Cholesky" | custom-call | tf_op jit(solution)/shard_map/cholesky/custom-call.1 | solution.py:63
  250.8 1.7 slice_add_fusion.1
  252.8 2.0 fusion.685
  260.0 11.7 %custom-call.23 = f32[128,128]{1,0:T(8,128)S(1)} custom-call(f32[128,128]{1,0:T(8,128)S(1)} %copy.361), custom_call_target="Cholesky" | custom-call | tf_op jit(solution)/shard_map/cholesky/custom-call.1 | solution.py:67
  275.9 3.1 fusion.33
  280.9 4.7 fusion.15
  286.0 11.7 %custom-call.24 = f32[128,128]{1,0:T(8,128)S(1)} custom-call(f32[128,128]{1,0:T(8,128)S(1)} %copy.371), custom_call_target="Cholesky" | custom-call | tf_op jit(solution)/shard_map/cholesky/custom-call.1 | solution.py:63
  302.1 11.9 %custom-call.25 = f32[128,128]{1,0:T(8,128)S(1)} custom-call(f32[128,128]{1,0:T(8,128)S(1)} %copy.375), custom_call_target="Cholesky" | custom-call | tf_op jit(solution)/shard_map/cholesky/custom-call.1 | solution.py:67
  318.1 2.3 fusion.41
  321.7 7.8 %all-gather.13.cloned.1.call-done = f32[32,256,1,256]{3,1,2,0:T(8,128)} async-done(((f32[1,256,1,256]{3,1,2,0:T(8,128)}), f32[32,256,1,256]{3,1,2,0:T(8,128)}) %all-gather.13.cloned.1.call-update) | async-done | bytes 8388624 | tf_op jit(solution)/shard_map/all_gather | solution.py:21
  329.5 1.9 slice.1536
  334.2 5.0 fusion.12
  339.7 11.7 %custom-call.26 = f32[128,128]{1,0:T(8,128)S(1)} custom-call(f32[128,128]{1,0:T(8,128)S(1)} %copy.385), custom_call_target="Cholesky" | custom-call | tf_op jit(solution)/shard_map/cholesky/custom-call.1 | solution.py:63
  356.4 11.7 %custom-call.27 = f32[128,128]{1,0:T(8,128)S(1)} custom-call(f32[128,128]{1,0:T(8,128)S(1)} %copy.389), custom_call_target="Cholesky" | custom-call | tf_op jit(solution)/shard_map/cholesky/custom-call.1 | solution.py:67
  372.1 1.8 fusion.55
  375.2 5.1 fusion.35
  380.7 12.1 %custom-call.28 = f32[128,128]{1,0:T(8,128)S(1)} custom-call(f32[128,128]{1,0:T(8,128)S(1)} %copy.396), custom_call_target="Cholesky" | custom-call | tf_op jit(solution)/shard_map/cholesky/custom-call.1 | solution.py:63
  397.6 11.7 %custom-call.29 = f32[128,128]{1,0:T(8,128)S(1)} custom-call(f32[128,128]{1,0:T(8,128)S(1)} %copy.400), custom_call_target="Cholesky" | custom-call | tf_op jit(solution)/shard_map/cholesky/custom-call.1 | solution.py:67
  415.3 4.9 fusion.43
  420.5 11.7 %custom-call.30 = f32[128,128]{1,0:T(8,128)S(1)} custom-call(f32[128,128]{1,0:T(8,128)S(1)} %copy.410), custom_call_target="Cholesky" | custom-call | tf_op jit(solution)/shard_map/cholesky/custom-call.1 | solution.py:63
  438.0 11.9 %custom-call.31 = f32[128,128]{1,0:T(8,128)S(1)} custom-call(f32[128,128]{1,0:T(8,128)S(1)} %fusion.504), custom_call_target="Cholesky" | custom-call | tf_op jit(solution)/shard_map/cholesky/custom-call.1 | solution.py:67
  455.7 4.2 fusion.48
  460.4 11.7 %custom-call.32 = f32[128,128]{1,0:T(8,128)S(1)} custom-call(f32[128,128]{1,0:T(8,128)S(1)} %copy.421), custom_call_target="Cholesky" | custom-call | tf_op jit(solution)/shard_map/cholesky/custom-call.1 | solution.py:63
  476.8 11.9 %custom-call.33 = f32[128,128]{1,0:T(8,128)S(1)} custom-call(f32[128,128]{1,0:T(8,128)S(1)} %broadcast_multiply_fusion.1), custom_call_target="Cholesky" | custom-call | tf_op jit(solution)/shard_map/cholesky/custom-call.1 | solution.py:67
  494.1 3.9 constant_dynamic-slice_fusion.3
  498.0 2.9 copy.428
  502.2 1.8 copy.430
  505.4 1.8 copy.432
  (483 shorter events, 116.6 us)
Async XLA Ops:
  6.5 85.0 %all-gather.9.cloned.1.call-start = ((), (), s32[]{:S(2)}) async-start(), calls=%async_computation | async-start | bytes 8650752 | tf_op jit(solution)/shard_map/all_gather | solution.py:21
  9.5 1.0 copy-start.4
  11.2 159.8 %all-gather.11.cloned.1.call-start = ((), (), s32[]{:S(2)}) async-start(), calls=%async_computation.1 | async-start | bytes 1310720 | tf_op jit(solution)/shard_map/all_gather | solution.py:105
  94.0 5.6 %copy-start = (f32[32,256,1,256]{3,1,2,0:T(8,128)S(1)}, f32[32,256,1,256]{3,1,2,0:T(8,128)}, u32[]{:S(2)}) copy-start(f32[32,256,1,256]{3,1,2,0:T(8,128)} %all-gather.9.cloned.1.call-done) | copy-start | bytes 25165828
  99.7 6.0 %copy-start.5 = (f32[2,256,2,256]{3,1,2,0:T(8,128)S(1)}, f32[2,256,2,256]{3,1,2,0:T(8,128)}, u32[]{:S(2)}) copy-start(f32[2,256,2,256]{3,1,2,0:T(8,128)} %copy-done.4) | copy-start | bytes 3145732
  117.5 0.7 copy-start.17
  131.5 4.3 copy-start.18
  132.9 2.0 copy-start.8
  135.2 0.6 copy-start.10
  142.1 2.0 copy-start.21
  143.8 14.8 %copy-start.11 = (f32[128,128]{1,0:T(8,128)S(1)}, f32[128,128]{1,0:T(8,128)}, u32[]{:S(2)}) copy-start(f32[128,128]{1,0:T(8,128)} %copy-done.10) | copy-start | bytes 196612
  143.8 109.0 %all-gather.15.cloned.1.call-start = ((), (), s32[]{:S(2)}) async-start(), calls=%async_computation.3 | async-start | bytes 1310720 | tf_op jit(solution)/shard_map/all_gather | solution.py:105
  157.9 2.4 copy-start.1
  159.8 169.7 %all-gather.13.cloned.1.call-start = ((), (), s32[]{:S(2)}) async-start(), calls=%async_computation.2 | async-start | bytes 8650752 | tf_op jit(solution)/shard_map/all_gather | solution.py:21
  160.0 1.9 copy-start.9
  160.1 1.9 copy-start.22
  171.0 2.2 copy-start.6
  179.6 0.7 copy-start.19
  192.1 3.7 copy-start.20
  222.2 3.7 copy-start.24
  225.9 3.4 copy-start.23
  229.3 2.2 copy-start.2
  229.3 2.2 copy-start.13
  235.6 0.7 copy-start.16
  252.5 4.1 copy-start.14
  279.0 1.9 copy-start.3
  372.1 3.1 copy-start.15
  394.6 2.6 copy-start.7
  412.7 2.6 copy-start.12
Sparse Core Ops, SparseCore 0:
  11.3 80.1 all-gather.8
  143.9 26.5 all-gather.10
  172.1 27.2 all-gather.14
  252.6 76.8 all-gather.12

commit v10 on v8

--- a/solution.py
+++ b/solution.py
@@ -109,7 +109,6 @@
     get_panel = separator_panels(working[:sep_slots], n_row, n_col, n_columns, gather_tail)
 
     total_rows = n_columns * tile + n_tail
-    factor = jnp.zeros((total_rows, n_columns * tile), jnp.float32)
     for k in range(n_columns):
         cols = slice(k * tile, (k + 1) * tile)
         if k == 0:
@@ -127,9 +126,9 @@
         lkk, linv = factor_diag(diag)
         below = mm(panel[tile:], linv.T)
         if k == 0:
-            factor = lax.dynamic_update_slice(factor, jnp.concatenate([lkk, below], axis=0), (0, 0))
             tail_below = mm(tail_pieces[0][0], linv.T)
-            factor = lax.dynamic_update_slice(factor, tail_below, (n_columns * tile, 0))
+            first = jnp.concatenate([lkk, below, tail_below], axis=0)
+            factor = jnp.pad(first, ((0, 0), (0, (n_columns - 1) * tile)))
         else:
             factor = factor.at[k * tile:, cols].set(jnp.concatenate([lkk, below], axis=0))
 

time: 516 us -> 519 us (level)
    pad x0 -> x1, local copies, waits for them, and re-layouts: none -> 8.98 us  [shards(): factor = jnp.pad(first, ((0, 0), (0, (n_columns - 1) * tile)))]
    dynamic_update_slice x1 -> x0, local copies, waits for them, and re-layouts: 8.93 us -> none  [shards(): lax.dynamic_update_slice(factor, jnp.concatenate([lkk, below], axis=0), (...]
    unnamed x53 -> x57, local copies, waits for them, and re-layouts: 19.1 us -> 19.1 us
where the time goes in v10:
time: 519 us; the launch traced here: 512 us
  other arithmetic  242 us (47%)
  waiting for transfers between devices  87.7 us (17%)
  matrix products  86.3 us (17%)
  local copies, waits for them, and re-layouts  76.2 us (15%)
  between operations  18.6 us (4%)
    another operation x24, other arithmetic, factor_diag(): l11 = jnp.tril(lax.linalg.cholesky(s11, symmetrize_input=True))  108 us
    another operation x24, other arithmetic, factor_diag(): lax.linalg.cholesky(diag[:half, :half], symmetrize_input=False)  101 us
    dot_general x160, matrix products, mm(): jnp.dot(a, b, precision=precision, preferred_element_type=jnp.float32)  86.3 us
    all_gather x2, waiting for transfers between devices, separator_panels(): pieces.append(lax.all_gather(piece, ('col', 'row'), axis=0))  80.2 us
    unnamed x57, local copies, waits for them, and re-layouts  19.1 us
    slice x7, local copies, waits for them, and re-layouts, panel(): pieces[k // n_col][base + k:base + n_row]  13.4 us
    reduce_sum x16, other arithmetic, lower_inverse(): diag = jnp.sum(lower * eye, axis=1)  11.5 us
  transfers between devices with their start and end apart: 4, of which 2 were waited for; matrix products, arithmetic and copies ran while one was open for 33% of the time, Pallas kernels for 0%

profile of v10, /device:TPU:0, one launch (start us, length us, event | category | flops | bytes accessed | tf_op | source)
XLA Modules:
  0.0 511.5 jit_solution(14728348025492122656)
XLA Ops:
  11.3 80.2 %all-gather.9.cloned.1.call-done = f32[32,256,1,256]{3,1,2,0:T(8,128)} async-done(((f32[1,256,1,256]{3,1,2,0:T(8,128)}), f32[32,256,1,256]{3,1,2,0:T(8,128)}) %all-gather.9.cloned.1.call-update) | async-done | bytes 8388624 | tf_op jit(solution)/shard_map/all_gather | solution.py:21
  91.5 2.5 slice.1434
  95.7 4.0 fusion.689
  99.7 4.8 copy.515
  108.5 1.8 copy.458
  114.5 1.8 copy.322
  118.9 12.5 %custom-call.18 = f32[128,128]{1,0:T(8,128)S(1)} custom-call(f32[128,128]{1,0:T(8,128)} %copy.323), custom_call_target="Cholesky" | custom-call | tf_op jit(solution)/shard_map/cholesky/custom-call.1 | solution.py:63
  137.5 2.8 copy.362
  140.3 1.7 copy.348
  142.0 1.7 copy.334
  144.3 11.7 %custom-call.19 = f32[128,128]{1,0:T(8,128)S(1)} custom-call(f32[128,128]{1,0:T(8,128)S(1)} %copy.327), custom_call_target="Cholesky" | custom-call | tf_op jit(solution)/shard_map/cholesky/custom-call.1 | solution.py:67
  160.3 2.9 fusion.105
  163.1 7.3 %all-gather.11.cloned.1.call-done = f32[4,256,1,256]{3,1,2,0:T(8,128)} async-done(((f32[1,256,1,256]{3,1,2,0:T(8,128)}), f32[4,256,1,256]{3,1,2,0:T(8,128)}) %all-gather.11.cloned.1.call-update) | async-done | bytes 1048592 | tf_op jit(solution)/shard_map/all_gather | solution.py:105
  170.5 1.9 fusion.691
  173.8 3.2 convolution_subtract_fusion
  177.4 11.7 %custom-call.20 = f32[128,128]{1,0:T(8,128)S(1)} custom-call(f32[128,128]{1,0:T(8,128)S(1)} %copy.338), custom_call_target="Cholesky" | custom-call | tf_op jit(solution)/shard_map/cholesky/custom-call.1 | solution.py:63
  193.7 20.4 %custom-call.21 = f32[128,128]{1,0:T(8,128)S(1)} custom-call(f32[128,128]{1,0:T(8,128)S(1)} %copy.342), custom_call_target="Cholesky" | custom-call | tf_op jit(solution)/shard_map/cholesky/custom-call.1 | solution.py:67
  218.3 4.2 fusion.31
  222.7 1.8 copy.517
  227.4 9.0 %pad.55 = f32[2304,2048]{1,0:T(8,128)} pad(f32[2304,256]{1,0:T(8,128)S(1)} %fusion.22, f32[]{:T(128)} %constant.324.clone.1), padding=0_0x0_1792 | pad | bytes 21233668 | tf_op jit(solution)/shard_map/jit(_pad)/pad | solution.py:131
  238.6 3.8 fusion.18
  243.5 11.9 %custom-call.22 = f32[128,128]{1,0:T(8,128)S(1)} custom-call(f32[128,128]{1,0:T(8,128)S(1)} %copy.352), custom_call_target="Cholesky" | custom-call | tf_op jit(solution)/shard_map/cholesky/custom-call.1 | solution.py:63
  260.4 1.8 copy.463
  262.2 1.8 copy.462
  265.6 11.7 %custom-call.23 = f32[128,128]{1,0:T(8,128)S(1)} custom-call(f32[128,128]{1,0:T(8,128)S(1)} %copy.356), custom_call_target="Cholesky" | custom-call | tf_op jit(solution)/shard_map/cholesky/custom-call.1 | solution.py:67
  281.4 3.1 fusion.36
  286.5 4.7 fusion.15
  291.5 11.7 %custom-call.24 = f32[128,128]{1,0:T(8,128)S(1)} custom-call(f32[128,128]{1,0:T(8,128)S(1)} %copy.366), custom_call_target="Cholesky" | custom-call | tf_op jit(solution)/shard_map/cholesky/custom-call.1 | solution.py:63
  307.7 11.9 %custom-call.25 = f32[128,128]{1,0:T(8,128)S(1)} custom-call(f32[128,128]{1,0:T(8,128)S(1)} %copy.370), custom_call_target="Cholesky" | custom-call | tf_op jit(solution)/shard_map/cholesky/custom-call.1 | solution.py:67
  323.7 2.3 fusion.44
  327.3 1.9 slice.1536
  332.0 5.0 fusion.12
  337.4 11.7 %custom-call.26 = f32[128,128]{1,0:T(8,128)S(1)} custom-call(f32[128,128]{1,0:T(8,128)S(1)} %copy.380), custom_call_target="Cholesky" | custom-call | tf_op jit(solution)/shard_map/cholesky/custom-call.1 | solution.py:63
  354.0 11.7 %custom-call.27 = f32[128,128]{1,0:T(8,128)S(1)} custom-call(f32[128,128]{1,0:T(8,128)S(1)} %copy.384), custom_call_target="Cholesky" | custom-call | tf_op jit(solution)/shard_map/cholesky/custom-call.1 | solution.py:67
  369.4 1.8 fusion.58
  372.5 5.1 fusion.38
  378.0 12.1 %custom-call.28 = f32[128,128]{1,0:T(8,128)S(1)} custom-call(f32[128,128]{1,0:T(8,128)S(1)} %copy.391), custom_call_target="Cholesky" | custom-call | tf_op jit(solution)/shard_map/cholesky/custom-call.1 | solution.py:63
  395.0 11.7 %custom-call.29 = f32[128,128]{1,0:T(8,128)S(1)} custom-call(f32[128,128]{1,0:T(8,128)S(1)} %copy.395), custom_call_target="Cholesky" | custom-call | tf_op jit(solution)/shard_map/cholesky/custom-call.1 | solution.py:67
  412.4 5.0 fusion.46
  417.8 11.7 %custom-call.30 = f32[128,128]{1,0:T(8,128)S(1)} custom-call(f32[128,128]{1,0:T(8,128)S(1)} %copy.405), custom_call_target="Cholesky" | custom-call | tf_op jit(solution)/shard_map/cholesky/custom-call.1 | solution.py:63
  435.3 11.9 %custom-call.31 = f32[128,128]{1,0:T(8,128)S(1)} custom-call(f32[128,128]{1,0:T(8,128)S(1)} %fusion.508), custom_call_target="Cholesky" | custom-call | tf_op jit(solution)/shard_map/cholesky/custom-call.1 | solution.py:67
  453.0 4.2 fusion.51
  457.6 11.7 %custom-call.32 = f32[128,128]{1,0:T(8,128)S(1)} custom-call(f32[128,128]{1,0:T(8,128)S(1)} %copy.416), custom_call_target="Cholesky" | custom-call | tf_op jit(solution)/shard_map/cholesky/custom-call.1 | solution.py:63
  474.1 11.9 %custom-call.33 = f32[128,128]{1,0:T(8,128)S(1)} custom-call(f32[128,128]{1,0:T(8,128)S(1)} %broadcast_multiply_fusion.1), custom_call_target="Cholesky" | custom-call | tf_op jit(solution)/shard_map/cholesky/custom-call.1 | solution.py:67
  491.4 3.9 constant_dynamic-slice_fusion.3
  495.3 2.9 copy.423
  499.5 1.9 copy.425
  502.8 1.8 copy.427
  (479 shorter events, 112.2 us)
Async XLA Ops:
  6.5 85.0 %all-gather.9.cloned.1.call-start = ((), (), s32[]{:S(2)}) async-start(), calls=%async_computation | async-start | bytes 8650752 | tf_op jit(solution)/shard_map/all_gather | solution.py:21
  9.5 1.0 copy-start.6
  11.2 159.3 %all-gather.11.cloned.1.call-start = ((), (), s32[]{:S(2)}) async-start(), calls=%async_computation.1 | async-start | bytes 1310720 | tf_op jit(solution)/shard_map/all_gather | solution.py:105
  94.0 5.6 %copy-start = (f32[32,256,1,256]{3,1,2,0:T(8,128)S(1)}, f32[32,256,1,256]{3,1,2,0:T(8,128)}, u32[]{:S(2)}) copy-start(f32[32,256,1,256]{3,1,2,0:T(8,128)} %all-gather.9.cloned.1.call-done) | copy-start | bytes 25165828
  99.7 6.0 %copy-start.7 = (f32[2,256,2,256]{3,1,2,0:T(8,128)S(1)}, f32[2,256,2,256]{3,1,2,0:T(8,128)}, u32[]{:S(2)}) copy-start(f32[2,256,2,256]{3,1,2,0:T(8,128)} %copy-done.6) | copy-start | bytes 3145732
  117.5 0.7 copy-start.19
  131.5 4.2 copy-start.20
  132.9 2.0 copy-start.10
  135.0 0.6 copy-start.12
  142.0 2.1 copy-start.21
  143.8 14.8 %copy-start.13 = (f32[128,128]{1,0:T(8,128)S(1)}, f32[128,128]{1,0:T(8,128)}, u32[]{:S(2)}) copy-start(f32[128,128]{1,0:T(8,128)} %copy-done.12) | copy-start | bytes 196612
  143.8 78.9 %all-gather.13.cloned.1.call-start = ((), (), s32[]{:S(2)}) async-start(), calls=%async_computation.2 | async-start | bytes 1310720 | tf_op jit(solution)/shard_map/all_gather | solution.py:105
  157.9 2.4 copy-start.2
  159.8 167.5 %all-gather.15.cloned.1.call-start = ((), (), s32[]{:S(2)}) async-start(), calls=%async_computation.3 | async-start | bytes 8650752 | tf_op jit(solution)/shard_map/all_gather | solution.py:21
  217.8 4.8 copy-start.1
  217.8 4.8 copy-start.11
  217.8 4.8 copy-start.22
  227.4 9.0 %copy-start.3 = (f32[1792,256]{1,0:T(8,128)S(1)}, f32[1792,256]{1,0:T(8,128)}, u32[]{:S(2)}) copy-start(f32[1792,256]{1,0:T(8,128)} %fusion.31) | copy-start | bytes 5505028
  236.4 2.2 copy-start.4
  242.4 15.7 %copy-start.8 = (f32[4,256,1,256]{3,1,2,0:T(8,128)S(1)}, f32[4,256,1,256]{3,1,2,0:T(8,128)}, u32[]{:S(2)}) copy-start(f32[4,256,1,256]{3,1,2,0:T(8,128)} %all-gather.13.cloned.1.call-done) | copy-start | bytes 3145732
  242.7 0.7 copy-start.17
  257.1 2.0 copy-start.15
  259.1 5.7 %copy-start.18 = (f32[256,256]{0,1:T(8,128)S(1)}, f32[256,256]{0,1:T(8,128)}, u32[]{:S(2)}) copy-start(f32[256,256]{0,1:T(8,128)} %copy-done.17) | copy-start | bytes 786436
  284.5 1.9 copy-start.5
  369.4 3.1 copy-start.16
  391.9 2.6 copy-start.9
  410.1 2.3 copy-start.14
Sparse Core Ops, SparseCore 0:
  11.3 80.1 all-gather.8
  143.9 26.5 all-gather.10
  172.1 27.5 all-gather.12
  227.5 77.5 all-gather.14
